TPU v7x, 8 devices: a whole 2x2x1 slice. The times are simulated.
8 devices in a mesh: dp: 2 (over z, y), tp: 4 (over x, core).
Axes of the slice: x: 2, y: 2, z: 1, core: 2. Of those that a mesh axis runs over, the one named last changes fastest.
Arguments:
- x_chunk: bfloat16 [64, 256, 1024], P('dp', 'tp'), parts along dimension 0
- prefix_len: int32 [64], P('dp'), parts along dimension 0
- k_cache: bfloat16 [64, 2048, 16, 64], P('dp', None, 'tp'), parts along dimension 0
- v_cache: bfloat16 [64, 2048, 16, 64], P('dp', None, 'tp'), parts along dimension 0
- ln1_gain: bfloat16 [1024], replicated
- ln1_bias: bfloat16 [1024], replicated
- w_qkv: bfloat16 [1024, 3072], P(None, 'tp')
- b_qkv: bfloat16 [3072], P('tp')
- w_out: bfloat16 [1024, 1024], P('tp')
- b_out: bfloat16 [1024], replicated
- ln2_gain: bfloat16 [1024], replicated
- ln2_bias: bfloat16 [1024], replicated
- w_up: bfloat16 [1024, 4096], P(None, 'tp')
- b_up: bfloat16 [4096], P('tp')
- w_down: bfloat16 [4096, 1024], P('tp')
- b_down: bfloat16 [1024], replicated
Outputs:
- output 1: bfloat16 [64, 256, 1024], P('dp', 'tp'), parts along dimension 0
- output 2: bfloat16 [64, 2048, 16, 64], P('dp', None, 'tp'), parts along dimension 0
- output 3: bfloat16 [64, 2048, 16, 64], P('dp', None, 'tp'), parts along dimension 0
There are 2 independent parts. A program takes and returns all parts, laid end to end along the dimension named above; an argument that names none is the same for every part.
All inputs are finite; a program needn't handle non-finite values.
Results may differ from a plain program's by a relative error of at most 0.0118672.
Values are sent between devices in bfloat16 or wider.
A program may use at most 1 GiB of HBM per device.

v0:
```python
import jax
import jax.numpy as jnp
from jax import lax
from jax.sharding import PartitionSpec as P

LN_EPS = 1e-5


def layer_norm(tok_rows, ln_gain, ln_bias):
    rows_f32 = tok_rows.astype(jnp.float32)
    row_mean = jnp.mean(rows_f32, axis=-1, keepdims=True)
    centered = rows_f32 - row_mean
    row_var = jnp.mean(centered * centered, axis=-1, keepdims=True)
    normed = centered * lax.rsqrt(row_var + LN_EPS)
    return (normed * ln_gain.astype(jnp.float32) + ln_bias.astype(jnp.float32)).astype(jnp.bfloat16)


def write_rows(cache_seq, new_rows, start_pos):
    zero_idx = jnp.zeros_like(start_pos)
    return lax.dynamic_update_slice(cache_seq, new_rows, (start_pos, zero_idx, zero_idx))


def attend(queries, k_upd, v_upd, prefix_len, head_offset, heads_all):
    batch_n, chunk_len, heads_loc, head_dim = queries.shape
    cache_len = k_upd.shape[1]
    scores = jnp.einsum('bchd,bthd->bhct', queries, k_upd, preferred_element_type=jnp.float32) * (head_dim ** -0.5)
    head_ids = head_offset + jnp.arange(heads_loc)
    slopes = jnp.exp2(-8.0 * (head_ids + 1).astype(jnp.float32) / heads_all)
    query_pos = prefix_len[:, None] + jnp.arange(chunk_len)[None, :]
    rel_pos = (jnp.arange(cache_len)[None, None, :] - query_pos[:, :, None]).astype(jnp.float32)
    scores = scores + slopes[None, :, None, None] * rel_pos[:, None]
    scores = jnp.where((rel_pos <= 0.0)[:, None], scores, -1e30)
    attn_probs = jax.nn.softmax(scores, axis=-1).astype(jnp.bfloat16)
    context = jnp.einsum('bhct,bthd->bchd', attn_probs, v_upd, preferred_element_type=jnp.float32)
    return context.astype(jnp.bfloat16).reshape(batch_n, chunk_len, heads_loc * head_dim)


def solution(mesh):
    tp_size = mesh.shape['tp']

    def local_layer(x_local, prefix_len, k_cache, v_cache, ln1_gain, ln1_bias, w_qkv, b_qkv, w_out, b_out, ln2_gain, ln2_bias, w_up, b_up, w_down, b_down):
        batch_n, tok_loc = x_local.shape[0], x_local.shape[1]
        heads_loc, head_dim = k_cache.shape[2], k_cache.shape[3]
        chunk_len = tok_loc * tp_size
        normed = layer_norm(x_local, ln1_gain, ln1_bias)
        gathered = lax.all_gather(normed, 'tp', axis=1, tiled=True)
        qkv_proj = jnp.einsum('bcd,de->bce', gathered, w_qkv, preferred_element_type=jnp.float32) + b_qkv.astype(jnp.float32)
        qkv_heads = qkv_proj.astype(jnp.bfloat16).reshape(batch_n, chunk_len, heads_loc, 3, head_dim)
        k_upd = jax.vmap(write_rows)(k_cache, qkv_heads[:, :, :, 1], prefix_len)
        v_upd = jax.vmap(write_rows)(v_cache, qkv_heads[:, :, :, 2], prefix_len)
        head_offset = lax.axis_index('tp') * heads_loc
        context = attend(qkv_heads[:, :, :, 0], k_upd, v_upd, prefix_len, head_offset, heads_loc * tp_size)
        attn_part = jnp.einsum('bce,ed->bcd', context, w_out, preferred_element_type=jnp.float32).astype(jnp.bfloat16)
        attn_sum = lax.psum_scatter(attn_part, 'tp', scatter_dimension=1, tiled=True)
        residual = (x_local.astype(jnp.float32) + attn_sum.astype(jnp.float32) + b_out.astype(jnp.float32)).astype(jnp.bfloat16)
        normed2 = layer_norm(residual, ln2_gain, ln2_bias)
        gathered2 = lax.all_gather(normed2, 'tp', axis=1, tiled=True)
        up_pre = jnp.einsum('bcd,df->bcf', gathered2, w_up, preferred_element_type=jnp.float32) + b_up.astype(jnp.float32)
        up_act = jax.nn.gelu(up_pre, approximate=True).astype(jnp.bfloat16)
        down_part = jnp.einsum('bcf,fd->bcd', up_act, w_down, preferred_element_type=jnp.float32).astype(jnp.bfloat16)
        down_sum = lax.psum_scatter(down_part, 'tp', scatter_dimension=1, tiled=True)
        x_out = (residual.astype(jnp.float32) + down_sum.astype(jnp.float32) + b_down.astype(jnp.float32)).astype(jnp.bfloat16)
        return x_out, k_upd, v_upd

    tok_spec = P('dp', 'tp', None)
    cache_spec = P('dp', None, 'tp', None)
    replicated = P()
    in_specs = (tok_spec, P('dp'), cache_spec, cache_spec, replicated, replicated, P(None, 'tp'), P('tp'), P('tp', None), replicated, replicated, replicated, P(None, 'tp'), P('tp'), P('tp', None), replicated)
    return jax.shard_map(local_layer, mesh=mesh, in_specs=in_specs, out_specs=(tok_spec, cache_spec, cache_spec), check_vma=False)
```

profile of v0, /device:TPU:0, one launch (start us, length us, event | category | flops | bytes accessed | tf_op | source)
XLA Modules:
  0.0 1576.2 jit_solution(9093774290587424232)
XLA Ops:
  7.2 23.0 %copy.44 = bf16[32,2048,4,64]{1,3,2,0:T(8,128)(2,1)} copy(bf16[32,2048,4,64]{1,3,2,0:T(8,128)(2,1)} %param.18) | data formatting | bytes 67108864
  30.3 22.9 %copy.45 = bf16[32,2048,4,64]{1,3,2,0:T(8,128)(2,1)} copy(bf16[32,2048,4,64]{1,3,2,0:T(8,128)(2,1)} %param.19) | data formatting | bytes 67108864
  59.1 4.6 fusion.36
  64.5 21.2 %subtract_convert_fusion = f32[32,256,2048]{2,1,0:T(8,128)} fusion(s32[32,256]{1,0:T(8,128)S(1)} %iota_add_fusion), kind=kLoop, calls=%fused_computation.17 | loop fusion | flops 33554432 | bytes 67141632 | tf_op jit(solution)/shard_map/convert_element_type | solution.py:30
  85.7 15.4 broadcast_compare_fusion
  101.1 69.8 %all-gather.3.cloned.1.call-done = bf16[32,256,1024]{2,1,0:T(8,128)(2,1)} async-done(((bf16[32,64,1024]{2,1,0:T(8,128)(2,1)}), bf16[32,256,1024]{2,1,0:T(8,128)(2,1)}) %all-gather.3.cloned.1.call-update) | async-done | bytes 16777232 | tf_op jit(solution)/shard_map/all_gather | solution.py:46
  170.9 19.9 %add_convert_fusion = bf16[32,256,768]{2,1,0:T(8,128)(2,1)} fusion(f32[768]{0:T(1024)S(1)} %convert_element_type.92, bf16[32,256,1024]{2,1,0:T(8,128)(2,1)} %all-gather.3.cloned.1.call-done, bf16[1024,768]{1,0:T(8,128)(2,1)} %param.22), kind=kOutput, calls=%fused_computation.29 | convolution fusion | flops 12897484800 | bytes 30936064 | tf_op jit(solution)/shard_map/bcd,de->bce/dot_general | solution.py:47
  190.8 16.7 %copy.23 = bf16[32,256,768]{1,2,0:T(8,128)(2,1)} copy(bf16[32,256,768]{2,1,0:T(8,128)(2,1)} %add_convert_fusion) | data formatting | bytes 25165824 | tf_op jit(solution)/shard_map/convert_element_type | solution.py:48
  207.4 6.1 slice_bitcast_fusion
  213.6 336.1 %while.3 = (s32[]{:T(128)}, bf16[32,2048,4,64]{1,3,2,0:T(8,128)(2,1)}, s32[32,4]{0,1:T(4,128)S(1)}, bf16[32,256,4,64]{1,3,2,0:T(8,128)(2,1)}, s32[]{:T(128)}, /*index=5*/s32[4]{0:T(128)S(1)}, s32[]{:T(128)}) while((s32[]{:T(128)}, bf16[32,2048,4,64]{1,3,2,0:T(8,128)(2,1)}, s32[32,4]{0,1:T(4,128)S(1)}, bf16[32,256,4,64]{1,3,2,0:T(8,128)(2,1)}, ...), condition=%wide.while_cond.1, body=%wide.while_body.1.sunk | while | flops 65565 | bytes 655555 | solution.py:20
  220.4 3.7 dynamic-update-slice.7
  230.9 3.7 dynamic-update-slice.7
  241.5 3.7 dynamic-update-slice.7
  252.0 3.7 dynamic-update-slice.7
  262.5 3.7 dynamic-update-slice.7
  273.1 3.7 dynamic-update-slice.7
  283.6 3.7 dynamic-update-slice.7
  294.1 3.7 dynamic-update-slice.7
  304.6 3.7 dynamic-update-slice.7
  315.2 3.7 dynamic-update-slice.7
  335.4 3.7 dynamic-update-slice.7
  345.9 3.7 dynamic-update-slice.7
  356.4 3.7 dynamic-update-slice.7
  367.0 3.7 dynamic-update-slice.7
  377.5 3.7 dynamic-update-slice.7
  388.0 3.7 dynamic-update-slice.7
  398.6 3.7 dynamic-update-slice.7
  409.1 3.7 dynamic-update-slice.7
  419.6 3.7 dynamic-update-slice.7
  430.2 3.7 dynamic-update-slice.7
  440.7 3.7 dynamic-update-slice.7
  451.2 3.7 dynamic-update-slice.7
  472.3 3.7 dynamic-update-slice.7
  493.3 3.7 dynamic-update-slice.7
  524.9 3.7 dynamic-update-slice.7
  549.7 336.6 %while.2 = (s32[]{:T(128)}, bf16[32,2048,4,64]{1,3,2,0:T(8,128)(2,1)}, s32[32,4]{0,1:T(4,128)S(1)}, bf16[32,256,4,64]{1,3,2,0:T(8,128)(2,1)}, s32[]{:T(128)}, /*index=5*/s32[4]{0:T(128)S(1)}, s32[]{:T(128)}) while((s32[]{:T(128)}, bf16[32,2048,4,64]{1,3,2,0:T(8,128)(2,1)}, s32[32,4]{0,1:T(4,128)S(1)}, bf16[32,256,4,64]{1,3,2,0:T(8,128)(2,1)}, ...), condition=%wide.while_cond, body=%wide.while_body.sunk | while | flops 65565 | bytes 655555 | solution.py:20
  556.5 3.7 dynamic-update-slice.6
  567.1 3.7 dynamic-update-slice.6
  598.7 3.7 dynamic-update-slice.6
  609.3 3.7 dynamic-update-slice.6
  619.8 3.7 dynamic-update-slice.6
  651.4 3.7 dynamic-update-slice.6
  682.2 3.7 dynamic-update-slice.6
  692.8 3.7 dynamic-update-slice.6
  724.4 3.7 dynamic-update-slice.6
  735.0 3.7 dynamic-update-slice.6
  745.5 3.7 dynamic-update-slice.6
  777.1 3.7 dynamic-update-slice.6
  787.7 3.7 dynamic-update-slice.6
  808.8 3.7 dynamic-update-slice.6
  819.3 3.7 dynamic-update-slice.6
  850.9 3.7 dynamic-update-slice.6
  861.5 3.7 dynamic-update-slice.6
  872.0 3.7 dynamic-update-slice.6
  886.3 157.4 %fusion.58 = (f32[32,4,256]{2,1,0:T(4,128)S(1)}, f32[32,4,256,2048]{3,2,1,0:T(8,128)}) fusion(f32[32,256,2048]{2,1,0:T(8,128)} %subtract_convert_fusion, f32[4]{0:T(128)S(1)} %multiply_exponential_fusion, pred[32,256,2048]{2,1,0:T(8,128)(4,1)} %broadcast_compare_fusion, bf16[32,2048,4,64]{1,3,2,0:T(8,128)(2,1)} %get-tuple-element.16, ...), kind=kOutput, calls=%fused_computation.83 | convolution fusion | flops 8992589824 | bytes 390201344 | tf_op jit(solution)/shard_map/sub | solution.py:33
  1043.8 93.3 %fusion.42 = bf16[32,4,64,256]{3,2,1,0:T(8,128)(2,1)} fusion(bf16[32,2048,4,64]{1,3,2,0:T(8,128)(2,1)} %get-tuple-element.8, f32[32,4,256,2048]{3,2,1,0:T(8,128)} %get-tuple-element.48, f32[32,4,256]{2,1,0:T(4,128)S(1)} %get-tuple-element.47), kind=kOutput, calls=%fused_computation.60 | convolution fusion | flops 8726249472 | bytes 306315264 | tf_op jit(solution)/shard_map/bhct,bthd->bchd/dot_general | solution.py:34
  1137.1 10.5 convolution_convert_fusion
  1147.9 118.5 %reduce-scatter.3.cloned.1.call-done = bf16[32,64,1024]{2,1,0:T(8,128)(2,1)} async-done(((bf16[32,256,1024]{2,1,0:T(8,128)(2,1)}), bf16[32,64,1024]{2,1,0:T(8,128)(2,1)}) %reduce-scatter.3.cloned.1.call-update) | async-done | bytes 4194320 | tf_op jit(solution)/shard_map/reduce_scatter | solution.py:54
  1266.5 5.0 convert_reduce_fusion
  1276.6 104.3 %all-gather.5.cloned.1.call-done = bf16[32,256,1024]{2,1,0:T(8,128)(2,1)} async-done(((bf16[32,64,1024]{2,1,0:T(8,128)(2,1)}), bf16[32,256,1024]{2,1,0:T(8,128)(2,1)}) %all-gather.5.cloned.1.call-update) | async-done | bytes 16777232 | tf_op jit(solution)/shard_map/all_gather | solution.py:57
  1380.9 34.2 %fusion.74 = bf16[32,256,1024]{2,1,0:T(8,128)(2,1)} fusion(f32[1024]{0:T(1024)S(1)} %convert_element_type.107, bf16[32,256,1024]{2,1,0:T(8,128)(2,1)} %all-gather.5.cloned.1.call-done, bf16[1024,1024]{1,0:T(8,128)(2,1)S(1)} %copy-done), kind=kOutput, calls=%fused_computation.26.clone.clone.clone.clone.1 | convolution fusion | flops 17263755264 | bytes 35655680 | tf_op jit(solution)/shard_map/bcd,df->bcf/dot_general | solution.py:58
  1415.1 27.5 %fusion.20 = bf16[32,256,1024]{2,1,0:T(8,128)(2,1)} fusion(bf16[1024,1024]{1,0:T(8,128)(2,1)} %param.30, bf16[32,256,1024]{2,1,0:T(8,128)(2,1)} %fusion.74), kind=kOutput, calls=%fused_computation.37 | convolution fusion | flops 17188257792 | bytes 35651584 | tf_op jit(solution)/shard_map/bcf,fd->bcd/dot_general | solution.py:60
  1443.3 118.2 %reduce-scatter.5.cloned.1.call-done = bf16[32,64,1024]{2,1,0:T(8,128)(2,1)} async-done(((bf16[32,256,1024]{2,1,0:T(8,128)(2,1)}), bf16[32,64,1024]{2,1,0:T(8,128)(2,1)}) %reduce-scatter.5.cloned.1.call-update) | async-done | bytes 4194320 | tf_op jit(solution)/shard_map/reduce_scatter | solution.py:61
  1561.6 7.9 fusion.40
  (335 shorter events, 524.6 us)
Async XLA Ops:
  7.2 1373.7 %copy-start = (bf16[1024,1024]{1,0:T(8,128)(2,1)S(1)}, bf16[1024,1024]{1,0:T(8,128)(2,1)}, u32[]{:S(2)}) copy-start(bf16[1024,1024]{1,0:T(8,128)(2,1)} %param.28) | copy-start | bytes 6291460
  7.2 163.7 %all-gather.3.cloned.1.call-start = ((), (), s32[]{:S(2)}) async-start(), calls=%async_computation.2 | async-start | bytes 20971520 | tf_op jit(solution)/shard_map/all_gather | solution.py:46
  30.3 28.8 %copy-start.4 = (bf16[1024]{0:T(1024)(128)(2,1)S(1)}, bf16[1024]{0:T(1024)(128)(2,1)}, u32[]{:S(2)}) copy-start(bf16[1024]{0:T(1024)(128)(2,1)} %param.20) | copy-start | bytes 6148
  30.3 28.8 %copy-start.5 = (bf16[1024]{0:T(1024)(128)(2,1)S(1)}, bf16[1024]{0:T(1024)(128)(2,1)}, u32[]{:S(2)}) copy-start(bf16[1024]{0:T(1024)(128)(2,1)} %param.21) | copy-start | bytes 6148
  53.2 11.1 copy-start.6
  53.2 11.1 copy-start.12
  53.2 11.1 copy-start.13
  63.7 1202.8 %reduce-scatter.3.cloned.1.call-start = ((), (), s32[]{:S(2)}) async-start(), calls=%async_computation.3 | async-start | bytes 20971520 | tf_op jit(solution)/shard_map/reduce_scatter | solution.py:54
  190.8 22.8 %copy-start.3 = (s32[4]{0:T(128)S(1)}, s32[4]{0:T(128)}, u32[]{:S(2)}) copy-start(s32[4]{0:T(128)} %constant.144) | copy-start | bytes 52
  1043.7 93.3 %copy-start.2 = (bf16[256,1024]{1,0:T(8,128)(2,1)S(1)}, bf16[256,1024]{1,0:T(8,128)(2,1)}, u32[]{:S(2)}) copy-start(bf16[256,1024]{1,0:T(8,128)(2,1)} %param.24) | copy-start | bytes 1572868
  1137.1 10.8 copy-start.7
  1137.1 10.8 copy-start.8
  1137.1 10.8 copy-start.9
  1147.6 129.0 %copy-start.10 = (bf16[1024]{0:T(1024)(128)(2,1)S(1)}, bf16[1024]{0:T(1024)(128)(2,1)}, u32[]{:S(2)}) copy-start(bf16[1024]{0:T(1024)(128)(2,1)} %param.29) | copy-start | bytes 6148
  1147.6 233.3 %all-gather.5.cloned.1.call-start = ((), (), s32[]{:S(2)}) async-start(), calls=%async_computation.4 | async-start | bytes 20971520 | tf_op jit(solution)/shard_map/all_gather | solution.py:57
  1271.5 2.0 copy-start.1
  1276.5 285.1 %reduce-scatter.5.cloned.1.call-start = ((), (), s32[]{:S(2)}) async-start(), calls=%async_computation.5 | async-start | bytes 20971520 | tf_op jit(solution)/shard_map/reduce_scatter | solution.py:61
  1442.6 0.7 copy-start.11
Sparse Core Ops, SparseCore 0:
  63.8 107.0 all-gather.2
  1147.7 118.7 reduce-scatter.2
  1276.6 104.1 all-gather.4
  1442.8 118.7 reduce-scatter.4
where the time goes:
time: 1590 us; the launch traced here: 1580 us
  other arithmetic  457 us (29%)
  waiting for transfers between devices  411 us (26%)
  local copies, waits for them, and re-layouts  349 us (22%)
  matrix products  343 us (22%)
    scatter x128, other arithmetic  393 us
    scatter x192, local copies, waits for them, and re-layouts  279 us
    sub x1, matrix products, attend(): attn_probs = jax.nn.softmax(scores, axis=-1).astype(jnp.bfloat16)  157 us
    reduce_scatter x1, waiting for transfers between devices, local_layer(): lax.psum_scatter(attn_part, 'tp', scatter_dimension=1, tiled=True)  119 us
    reduce_scatter x1, waiting for transfers between devices, local_layer(): lax.psum_scatter(down_part, 'tp', scatter_dimension=1, tiled=True)  118 us
    all_gather x1, waiting for transfers between devices, local_layer(): gathered2 = lax.all_gather(normed2, 'tp', axis=1, tiled=True)  104 us
    dot_general x1, matrix products, attend(): jnp.einsum('bhct,bthd->bchd', attn_probs, v_upd, preferred_element_type=j...  93.3 us
    all_gather x1, waiting for transfers between devices, local_layer(): gathered = lax.all_gather(normed, 'tp', axis=1, tiled=True)  69.8 us
  transfers between devices with their start and end apart: 4, of which 4 were waited for; matrix products, arithmetic and copies ran while one was open for 2% of the time, Pallas kernels for 0%

commit v1 on v0

v1 whole, which is shorter than its diff:
```python
import functools

import jax
import jax.numpy as jnp
from jax import lax
from jax.experimental import pallas as pl
from jax.experimental.pallas import tpu as pltpu
from jax.sharding import PartitionSpec as P

LN_EPS = 1e-5
LOG2E = 1.4426950408889634
NEG = -1e30
NCHUNK = 4
KB = 256
XOR1 = [(0, 1), (1, 0), (2, 3), (3, 2)]
XOR2 = [(0, 2), (2, 0), (1, 3), (3, 1)]
XOR3 = [(0, 3), (3, 0), (1, 2), (2, 1)]
HBM = pltpu.HBM


def norm_rows(rows_f32, gain, bias):
    row_mean = jnp.mean(rows_f32, axis=-1, keepdims=True)
    centered = rows_f32 - row_mean
    row_var = jnp.mean(centered * centered, axis=-1, keepdims=True)
    normed = centered * lax.rsqrt(row_var + LN_EPS)
    return (normed * gain + bias).astype(jnp.bfloat16)


def ln_kernel(x_ref, gain_ref, bias_ref, o_ref):
    rows = x_ref[...].reshape(-1, x_ref.shape[-1]).astype(jnp.float32)
    gain = gain_ref[...].astype(jnp.float32)
    bias = bias_ref[...].astype(jnp.float32)
    o_ref[...] = norm_rows(rows, gain, bias).reshape(o_ref.shape)


def layer_norm_chunk(x, gain, bias, start, count):
    tok, dim = x.shape[1], x.shape[2]
    step = 4
    return pl.pallas_call(
        ln_kernel,
        grid=(count // step,),
        in_specs=[
            pl.BlockSpec((step, tok, dim), lambda i: (start // step + i, 0, 0)),
            pl.BlockSpec((1, dim), lambda i: (0, 0)),
            pl.BlockSpec((1, dim), lambda i: (0, 0)),
        ],
        out_specs=pl.BlockSpec((step, tok, dim), lambda i: (i, 0, 0)),
        out_shape=jax.ShapeDtypeStruct((count, tok, dim), jnp.bfloat16),
        cost_estimate=pl.CostEstimate(flops=count * tok * dim * 10, bytes_accessed=count * tok * dim * 4, transcendentals=0),
        name='ln1',
    )(x, gain, bias)


def attn_kernel(start, meta_ref, slope_ref, a0, a1, a2, a3, w_ref, b_ref, kc_ref, vc_ref, *rest):
    has_prev = start > 0
    if has_prev:
        rest = rest[2:]
    c0, c1, c2, c3, ko_ref, vo_ref, a_scr, qkv_scr, bias_scr, m_scr, acc_scr, ctx_scr = rest
    heads, hd, cache_len = kc_ref.shape[1:]
    tok = a0.shape[1]
    chunk = 4 * tok
    tp = meta_ref[0]
    step = pl.program_id(0)
    pos = meta_ref[1 + start + step]

    diff = (lax.broadcasted_iota(jnp.int32, (KB, chunk), 0) - lax.broadcasted_iota(jnp.int32, (KB, chunk), 1))

    @pl.when(step == 0)
    def _():
        for h in range(heads):
            bias_scr[h] = diff.astype(jnp.float32) * (slope_ref[h] * LOG2E)

    for k, blk in enumerate((a0, a1, a2, a3)):
        a_scr[pl.ds(pl.multiple_of((tp ^ k) * tok, tok), tok), :] = blk[0]
    qkv = lax.dot_general(w_ref[...], a_scr[...], (((1,), (1,)), ((), ())), preferred_element_type=jnp.float32)
    qkv = qkv + b_ref[...]
    qkv_scr[...] = qkv.astype(jnp.bfloat16)

    ko_ref[...] = kc_ref[...]
    vo_ref[...] = vc_ref[...]
    win = chunk + 128
    base = pl.multiple_of(jnp.minimum((pos // 128) * 128, cache_len - win), 128)
    off = pos - base
    lane = lax.broadcasted_iota(jnp.int32, (hd, win), 1)
    inside = (lane >= off) & (lane < off + chunk)
    pad = jnp.zeros((hd, 128), jnp.float32)
    for h in range(heads):
        for part, dst in ((1, ko_ref), (2, vo_ref)):
            row = h * 3 * hd + part * hd
            new = qkv_scr[row:row + hd, :].astype(jnp.float32)
            new = pltpu.roll(jnp.concatenate([new, pad], axis=1), off, 1)
            old = dst[0, h, :, pl.ds(base, win)].astype(jnp.float32)
            dst[0, h, :, pl.ds(base, win)] = jnp.where(inside, new, old).astype(jnp.bfloat16)

    m_scr[...] = jnp.full_like(m_scr, NEG)
    acc_scr[...] = jnp.zeros_like(acc_scr)
    ones = jnp.ones((16, KB), jnp.bfloat16)

    def block(kb, masked):
        j0 = pl.multiple_of(kb * KB, KB)
        for h in range(heads):
            keys = ko_ref[0, h, :, pl.ds(j0, KB)]
            vals = jnp.concatenate([vo_ref[0, h, :, pl.ds(j0, KB)], ones], axis=0)
            q = qkv_scr[h * 3 * hd:h * 3 * hd + hd, :]
            s = lax.dot_general(keys, q, (((0,), (0,)), ((), ())), preferred_element_type=jnp.float32)
            s = s * (LOG2E * hd ** -0.5) + bias_scr[h]
            if masked:
                s = jnp.where(diff <= pos - j0, s, NEG)
            shift = slope_ref[h] * LOG2E * (j0 - pos).astype(jnp.float32)
            m_old = m_scr[h]
            m_new = jnp.maximum(m_old, jnp.max(s, axis=0, keepdims=True) + shift)
            p = jnp.exp2(s - (m_new - shift)).astype(jnp.bfloat16)
            alpha = jnp.exp2(m_old - m_new)
            m_scr[h] = m_new
            acc_scr[h] = acc_scr[h] * alpha + jnp.dot(vals, p, preferred_element_type=jnp.float32)

    full = pos // KB
    total = (pos + chunk + KB - 1) // KB
    lax.fori_loop(0, full, lambda kb, c: (block(kb, False), c)[1], 0)
    lax.fori_loop(full, total, lambda kb, c: (block(kb, True), c)[1], 0)

    for h in range(heads):
        ctx = acc_scr[h, :hd, :] / acc_scr[h, hd:hd + 1, :]
        ctx_scr[:, h * hd:(h + 1) * hd] = ctx.T.astype(jnp.bfloat16)
    for k, out in enumerate((c0, c1, c2, c3)):
        out[0] = ctx_scr[pl.ds(pl.multiple_of((tp ^ k) * tok, tok), tok), :]


def attention_chunk(meta, slopes, blocks, w_t, b_col, k_t, v_t, prev, start):
    count, tok, dim = blocks[0].shape
    heads, hd, cache_len = k_t.shape[1:]
    chunk = 4 * tok
    cols = heads * hd
    tok_spec = pl.BlockSpec((1, tok, dim), lambda i, *_: (i, 0, 0))
    cache_spec = pl.BlockSpec((1, heads, hd, cache_len), lambda i, *_: (start + i, 0, 0, 0))
    any_spec = pl.BlockSpec(memory_space=pl.ANY)
    in_specs = [tok_spec] * 4 + [
        pl.BlockSpec(w_t.shape, lambda i, *_: (0, 0)),
        pl.BlockSpec(b_col.shape, lambda i, *_: (0, 0)),
        cache_spec, cache_spec]
    operands = [*blocks, w_t, b_col, k_t, v_t]
    aliases = {}
    if prev is not None:
        in_specs += [any_spec, any_spec]
        operands += list(prev)
        aliases = {2 + 8: 4, 2 + 9: 5}
    ctx_spec = pl.BlockSpec((1, tok, cols), lambda i, *_: (i, 0, 0))
    return pl.pallas_call(
        functools.partial(attn_kernel, start),
        grid_spec=pltpu.PrefetchScalarGridSpec(
            num_scalar_prefetch=2,
            grid=(count,),
            in_specs=in_specs,
            out_specs=[ctx_spec] * 4 + [cache_spec, cache_spec],
            scratch_shapes=[
                pltpu.VMEM((chunk, dim), jnp.bfloat16),
                pltpu.VMEM((3 * cols, chunk), jnp.bfloat16),
                pltpu.VMEM((heads, KB, chunk), jnp.float32),
                pltpu.VMEM((heads, 1, chunk), jnp.float32),
                pltpu.VMEM((heads, hd + 16, chunk), jnp.float32),
                pltpu.VMEM((chunk, cols), jnp.bfloat16),
            ]),
        out_shape=[jax.ShapeDtypeStruct((count, tok, cols), jnp.bfloat16)] * 4
        + [jax.ShapeDtypeStruct(k_t.shape, k_t.dtype)] * 2,
        input_output_aliases=aliases,
        cost_estimate=pl.CostEstimate(
            flops=count * 20 * 500_000_000, bytes_accessed=count * 4 * heads * hd * cache_len * 2, transcendentals=0),
        compiler_params=pltpu.CompilerParams(vmem_limit_bytes=40 * 1024 * 1024),
        name='attn',
    )(meta, slopes, *operands)


def mlp_kernel(start, rows, *refs):
    c0, c1, c2, c3, x_ref, bo_ref, g2_ref, b2_ref, bu0, bu1, bu2, bu3, bd_ref = refs[:13]
    wo_hbm = refs[13:17]
    wu_hbm = refs[17:21]
    wd_hbm = refs[21:25]
    rest = refs[25:]
    if start > 0:
        rest = rest[1:]
    o_ref, wo, wu, wd, sem_o, sem_u, sem_d, n_scr, r_scr, h_scr, y_scr = rest
    dim = x_ref.shape[-1]

    def copies(k):
        return (pltpu.make_async_copy(wo_hbm[k], wo.at[k], sem_o.at[k]),
                pltpu.make_async_copy(wu_hbm[k], wu.at[k], sem_u.at[k]),
                pltpu.make_async_copy(wd_hbm[k], wd.at[k], sem_d.at[k]))

    for k in range(4):
        copies(k)[0].start()
    for k in range(4):
        copies(k)[1].start()
        copies(k)[2].start()

    y = None
    for k, c in enumerate((c0, c1, c2, c3)):
        copies(k)[0].wait()
        part = jnp.dot(c[...].reshape(rows, -1), wo[k], preferred_element_type=jnp.float32)
        y = part if y is None else y + part
    r = (x_ref[...].reshape(rows, dim).astype(jnp.float32) + y + bo_ref[...].astype(jnp.float32)).astype(jnp.bfloat16)
    r_scr[...] = r
    n_scr[...] = norm_rows(r.astype(jnp.float32), g2_ref[...].astype(jnp.float32), b2_ref[...].astype(jnp.float32))
    for k, bu in enumerate((bu0, bu1, bu2, bu3)):
        copies(k)[1].wait()
        copies(k)[2].wait()
        up = jnp.dot(n_scr[...], wu[k], preferred_element_type=jnp.float32) + bu[...].astype(jnp.float32)
        h_scr[...] = jax.nn.gelu(up, approximate=True).astype(jnp.bfloat16)
        down = jnp.dot(h_scr[...], wd[k], preferred_element_type=jnp.float32)
        if k == 0:
            y_scr[...] = down
        elif k < 3:
            y_scr[...] += down
        else:
            out = r_scr[...].astype(jnp.float32) + (y_scr[...] + down) + bd_ref[...].astype(jnp.float32)
            o_ref[...] = out.astype(jnp.bfloat16).reshape(o_ref.shape)


def mlp_chunk(ctx, x, small, wo, wu, wd, prev, start):
    count, tok, cols = ctx[0].shape
    dim = x.shape[2]
    rows = count * tok
    hid = wu[0].shape[1]
    whole = lambda a: pl.BlockSpec(a.shape, lambda i: (0,) * a.ndim)
    any_spec = pl.BlockSpec(memory_space=pl.ANY)
    x_spec = pl.BlockSpec((count, tok, dim), lambda i: (start // count, 0, 0))
    in_specs = [whole(c) for c in ctx] + [x_spec] + [whole(a) for a in small] + [any_spec] * 12
    operands = [*ctx, x, *small, *wo, *wu, *wd]
    aliases = {}
    if prev is not None:
        aliases = {len(operands): 0}
        in_specs.append(any_spec)
        operands.append(prev)
    return pl.pallas_call(
        functools.partial(mlp_kernel, start, rows),
        grid=(1,),
        in_specs=in_specs,
        out_specs=x_spec,
        out_shape=jax.ShapeDtypeStruct(x.shape, x.dtype),
        scratch_shapes=[
            pltpu.VMEM((4, cols, dim), jnp.bfloat16),
            pltpu.VMEM((4, dim, hid), jnp.bfloat16),
            pltpu.VMEM((4, hid, dim), jnp.bfloat16),
            pltpu.SemaphoreType.DMA((4,)),
            pltpu.SemaphoreType.DMA((4,)),
            pltpu.SemaphoreType.DMA((4,)),
            pltpu.VMEM((rows, dim), jnp.bfloat16),
            pltpu.VMEM((rows, dim), jnp.bfloat16),
            pltpu.VMEM((rows, hid), jnp.bfloat16),
            pltpu.VMEM((rows, dim), jnp.float32),
        ],
        input_output_aliases=aliases,
        cost_estimate=pl.CostEstimate(
            flops=20 * rows * 9 * dim * dim * 2, bytes_accessed=rows * dim * 8 + 18 * dim * dim, transcendentals=0),
        compiler_params=pltpu.CompilerParams(vmem_limit_bytes=52 * 1024 * 1024),
        name='mlp',
    )(*operands)


def solution(mesh):
    tp_size = mesh.shape['tp']

    def local_layer(x, prefix_len, k_cache, v_cache, ln1_gain, ln1_bias, w_qkv, b_qkv, w_out, b_out, ln2_gain, ln2_bias, w_up, b_up, w_down, b_down):
        batch = x.shape[0]
        heads = k_cache.shape[2]
        count = batch // NCHUNK
        tp = lax.axis_index('tp')
        row = lambda a: a.reshape(1, -1)
        perm = lambda a, pairs: lax.ppermute(a, 'tp', pairs)

        def gather(a):
            near, far = perm(a, XOR1), perm(a, XOR2)
            return [a, near, far, perm(far, XOR1)]

        normed = [layer_norm_chunk(x, row(ln1_gain), row(ln1_bias), c * count, count) for c in range(NCHUNK)]
        blocks = [gather(n) for n in normed]
        wo, wu, wd, bu = gather(w_out), gather(w_up), gather(w_down), gather(row(b_up))

        meta = jnp.concatenate([tp[None].astype(jnp.int32), prefix_len])
        head_ids = tp * heads + jnp.arange(heads)
        slopes = jnp.exp2(-8.0 * (head_ids + 1).astype(jnp.float32) / (heads * tp_size))
        w_t = w_qkv.T
        b_col = b_qkv.astype(jnp.float32).reshape(-1, 1)
        k_t = k_cache.transpose(0, 2, 3, 1)
        v_t = v_cache.transpose(0, 2, 3, 1)
        small = [row(b_out), row(ln2_gain), row(ln2_bias), *bu, row(b_down)]

        caches, x_out = None, None
        sent = []
        for c in range(NCHUNK):
            outs = attention_chunk(meta, slopes, blocks[c], w_t, b_col, k_t, v_t, caches, c * count)
            caches = outs[4:]
            sent.append([outs[0], perm(outs[1], XOR1), perm(outs[2], XOR2), perm(outs[3], XOR3)])
        for c in range(NCHUNK):
            x_out = mlp_chunk(sent[c], x, small, wo, wu, wd, x_out, c * count)
        return x_out, caches[0].transpose(0, 3, 1, 2), caches[1].transpose(0, 3, 1, 2)

    tok_spec = P('dp', 'tp', None)
    cache_spec = P('dp', None, 'tp', None)
    replicated = P()
    in_specs = (tok_spec, P('dp'), cache_spec, cache_spec, replicated, replicated, P(None, 'tp'), P('tp'), P('tp', None), replicated, replicated, replicated, P(None, 'tp'), P('tp'), P('tp', None), replicated)
    return jax.shard_map(local_layer, mesh=mesh, in_specs=in_specs, out_specs=(tok_spec, cache_spec, cache_spec), check_vma=False)
```

time: 1590 us -> 448 us (0.28); the launches traced: 1580 us -> 453 us
  other arithmetic: 457 us -> 0.08 us
  Pallas kernels: 0 us -> 354 us
  local copies, waits for them, and re-layouts: 349 us -> 4.97 us
  matrix products: 343 us -> 0 us
  waiting for transfers between devices: 411 us -> 68.8 us
  starting transfers between devices: 0.9 us -> 23 us
    scatter x129 -> x0, other arithmetic: 393 us -> none
    pallas_call x0 -> x12, Pallas kernels: none -> 354 us  [the longest x4 269 us: attention_chunk(): pl.pallas_call(functools.partial(attn_kernel, start), grid_spec=pltpu.Pre...]
    scatter x192 -> x0, local copies, waits for them, and re-layouts: 279 us -> none
    reduce_scatter x2 -> x0, waiting for transfers between devices: 237 us -> none  [the longest x1 119 us: local_layer(): lax.psum_scatter(attn_part, 'tp', scatter_dimension=1, tiled=True)]
    dot_general x5 -> x0, matrix products: 185 us -> none  [the longest x1 93.3 us: attend(): jnp.einsum('bhct,bthd->bchd', attn_probs, v_upd, preferred_element_type=j...]
    all_gather x2 -> x0, waiting for transfers between devices: 174 us -> none  [the longest x1 104 us: local_layer(): gathered2 = lax.all_gather(normed2, 'tp', axis=1, tiled=True)]
    sub x1 -> x0, matrix products: 157 us -> none  [attend(): attn_probs = jax.nn.softmax(scores, axis=-1).astype(jnp.bfloat16)]
    ppermute x0 -> x36, waiting for transfers between devices: none -> 68.8 us  [local_layer(): perm = lambda a, pairs: lax.ppermute(a, 'tp', pairs)]
  transfers between devices with their start and end apart: 4 -> 36, of which waited for: 4 -> 3; matrix products, arithmetic and copies ran while one was open for 2% -> 0% of each run, Pallas kernels for 0% -> 73%
where the time goes in v1:
time: 448 us; the launch traced here: 453 us
  Pallas kernels  354 us (79%)
  waiting for transfers between devices  68.8 us (15%)
  starting transfers between devices  23 us (5%)
  local copies, waits for them, and re-layouts  4.97 us (1%)
    pallas_call x4, Pallas kernels, attention_chunk(): pl.pallas_call(functools.partial(attn_kernel, start), grid_spec=pltpu.Pre...  269 us
    pallas_call x4, Pallas kernels, mlp_chunk(): pl.pallas_call(functools.partial(mlp_kernel, start, rows), grid=(1,), in_...  75.1 us
    ppermute x36, waiting for transfers between devices, local_layer(): perm = lambda a, pairs: lax.ppermute(a, 'tp', pairs)  68.8 us
    ppermute x36, starting transfers between devices, local_layer(): perm = lambda a, pairs: lax.ppermute(a, 'tp', pairs)  23 us
    pallas_call x4, Pallas kernels, layer_norm_chunk(): pl.pallas_call(ln_kernel, grid=(count // step,), in_specs=[pl.BlockSpec((...  10.8 us
  transfers between devices with their start and end apart: 36, of which 3 were waited for; matrix products, arithmetic and copies ran while one was open for 0% of the time, Pallas kernels for 73%

profile of v1, /device:TPU:0, one launch (start us, length us, event | category | flops | bytes accessed | tf_op | source)
XLA Modules:
  0.0 452.8 jit_solution(10675057831869322320)
XLA Ops:
  0.6 1.3 reshape.38.gain_ref
  1.9 1.3 reshape.39.bias_ref
  3.2 2.8 ln1.7.a0
  6.0 0.0 copy-start.9
  6.0 0.0 copy-start.10
  6.0 3.4 collective-permute-start.10
  9.4 2.6 ln1.6.a0
  12.0 0.0 collective-permute-start.7
  12.0 21.3 %collective-permute-done.10.a2 = bf16[8,64,1024]{2,1,0:T(8,128)(2,1)} collective-permute-done((bf16[8,64,1024]{2,1,0:T(8,128)(2,1)}, bf16[8,64,1024]{2,1,0:T(8,128)(2,1)}, u32[]{:S(2)}, u32[]{:S(2)}) %collective-permute-start.10) | collective-permute-done | bytes 1048608 | tf_op jit(solution)/shard_map/ppermute | solution.py:268
  33.4 0.5 collective-permute-start.15
  33.9 2.0 collective-permute-start.16
  35.9 19.1 %collective-permute-done.16.refs_10_ = bf16[1,1024]{1,0:T(2,128)(2,1)S(1)} collective-permute-done((bf16[1,1024]{1,0:T(2,128)(2,1)S(1)}, bf16[1,1024]{1,0:T(2,128)(2,1)S(1)}, u32[]{:S(2)}, u32[]{:S(2)}) %collective-permute-start.16) | collective-permute-done | bytes 2080 | tf_op jit(solution)/shard_map/ppermute | solution.py:268
  55.1 0.0 collective-permute-start.17
  55.1 0.1 pad_add_fusion.meta_ref
  55.2 0.8 copy.29
  55.9 0.2 reshape.49.b_ref
  56.2 0.0 copy-start.1
  56.2 2.7 ln1.4.a0
  58.9 2.7 ln1.5.a0
  61.6 0.5 collective-permute-start.6
  62.1 0.0 collective-permute-done.17.refs_11_
  62.1 0.0 collective-permute-start.18
  62.2 0.0 collective-permute-done.7.a2
  62.2 1.7 collective-permute-start.19
  63.9 0.0 collective-permute-done.9.a1
  63.9 0.3 collective-permute-start.4
  64.2 0.0 collective-permute-done.11.a3
  64.2 70.5 %attn.4 = (bf16[8,64,256]{2,1,0:T(8,128)(2,1)S(1)}, bf16[8,64,256]{2,1,0:T(8,128)(2,1)S(1)}, bf16[8,64,256]{2,1,0:T(8,128)(2,1)S(1)}, bf16[8,64,256]{2,1,0:T(8,1...) custom-call(s32[33]{0:T(128)S(1)} %pad_add_fusion.meta_ref, ...), custom_call_target="tpu_custom_call" | custom-call | flops 80000000000 | bytes 33554432 | tf_op jit(solution)/shard_map/attn/pallas_call | solution.py:148
  134.8 0.0 collective-permute-done.18.refs_14_
  134.8 0.5 collective-permute-start
  135.3 0.0 collective-permute-done.19.refs_15_
  135.3 1.7 collective-permute-start.1
  137.0 0.0 collective-permute-done.4.a2
  137.1 0.0 collective-permute-done.6.a1
  137.1 0.5 collective-permute-start.20
  137.6 0.0 collective-permute-done.8.a3
  137.6 0.0 collective-permute-start.5
  137.6 69.4 %attn.5 = (bf16[8,64,256]{2,1,0:T(8,128)(2,1)S(1)}, bf16[8,64,256]{2,1,0:T(8,128)(2,1)}, bf16[8,64,256]{2,1,0:T(8,128)(2,1)}, bf16[8,64,256]{2,1,0:T(8,128)(2,1)...) custom-call(s32[33]{0:T(128)S(1)} %pad_add_fusion.meta_ref, ...), custom_call_target="tpu_custom_call", output_to_operand_aliasing={{4}: (10, {}), {5}: (11, {})} | custom-call | flops 80000000000 | bytes 33554432 | tf_op jit(solution)/shard_map/attn/pallas_call | solution.py:148
  207.0 0.0 collective-permute-done.a1
  207.0 0.5 collective-permute-start.21
  207.5 0.0 collective-permute-done.1.a2
  207.5 0.3 collective-permute-start.22
  207.8 0.0 collective-permute-done.3.a1
  207.9 1.7 collective-permute-start.25
  209.6 0.2 collective-permute-start.2
  209.8 60.4 %attn.6 = (bf16[8,64,256]{2,1,0:T(8,128)(2,1)S(1)}, bf16[8,64,256]{2,1,0:T(8,128)(2,1)}, bf16[8,64,256]{2,1,0:T(8,128)(2,1)}, bf16[8,64,256]{2,1,0:T(8,128)(2,1)...) custom-call(s32[33]{0:T(128)S(1)} %pad_add_fusion.meta_ref, ...), custom_call_target="tpu_custom_call", output_to_operand_aliasing={{4}: (10, {}), {5}: (11, {})} | custom-call | flops 80000000000 | bytes 33554432 | tf_op jit(solution)/shard_map/attn/pallas_call | solution.py:148
  270.2 0.3 collective-permute-start.33
  270.5 0.8 collective-permute-start.34
  271.3 0.7 collective-permute-start.35
  272.1 0.6 collective-permute-start.23
  272.7 28.3 %collective-permute-done.25.refs_23_ = bf16[1024,1024]{1,0:T(8,128)(2,1)} collective-permute-done((bf16[1024,1024]{1,0:T(8,128)(2,1)S(1)}, bf16[1024,1024]{1,0:T(8,128)(2,1)}, u32[]{:S(2)}, u32[]{:S(2)}) %collective-permute-start.25) | collective-permute-done | bytes 2097184 | tf_op jit(solution)/shard_map/ppermute | solution.py:268
  301.0 68.2 %attn.7 = (bf16[8,64,256]{2,1,0:T(8,128)(2,1)S(1)}, bf16[8,64,256]{2,1,0:T(8,128)(2,1)}, bf16[8,64,256]{2,1,0:T(8,128)(2,1)}, bf16[8,64,256]{2,1,0:T(8,128)(2,1)...) custom-call(s32[33]{0:T(128)S(1)} %pad_add_fusion.meta_ref, ...), custom_call_target="tpu_custom_call", output_to_operand_aliasing={{4}: (10, {}), {5}: (11, {})} | custom-call | flops 80000000000 | bytes 33554432 | tf_op jit(solution)/shard_map/attn/pallas_call | solution.py:148
  369.2 0.5 collective-permute-start.12
  369.8 0.3 collective-permute-start.13
  370.1 1.4 copy-done.15
  371.5 1.7 collective-permute-start.31
  373.2 0.2 collective-permute-start.32
  373.4 18.4 %mlp.4.refs_25_ = bf16[32,64,1024]{2,1,0:T(8,128)(2,1)} custom-call(bf16[8,64,256]{2,1,0:T(8,128)(2,1)S(1)} %get-tuple-element.45.refs_0_, bf16[8,64,256]{2,1,0:T(8,128)(2,1)S(1)} %collective-permute-done.33.refs_1_, bf16[8,64,256]{2,1,0:T(8,128)(2,1)S(1)} %collective-permute-done.34.refs_2_, bf16[8,64,256]{2,1,0:T(8,128)(2,1)S(1)} %collective-permute-done.35.refs_3_, ...), custom_call_target="tpu_custom_call" | custom-call | flops 193273528320 | bytes 23068672 | tf_op jit(solution)/shard_map/mlp/pallas_call | solution.py:233
  391.8 0.3 collective-permute-start.27
  392.1 1.7 collective-permute-start.28
  393.8 18.9 %mlp.5.refs_25_ = bf16[32,64,1024]{2,1,0:T(8,128)(2,1)} custom-call(bf16[8,64,256]{2,1,0:T(8,128)(2,1)S(1)} %get-tuple-element.41.refs_0_, bf16[8,64,256]{2,1,0:T(8,128)(2,1)} %collective-permute-done.30.refs_1_, bf16[8,64,256]{2,1,0:T(8,128)(2,1)} %collective-permute-done.31.refs_2_, ...), custom_call_target="tpu_custom_call", output_to_operand_aliasing={{}: (25, {})} | custom-call | flops 193273528320 | bytes 23068672 | tf_op jit(solution)/shard_map/mlp/pallas_call | solution.py:233
  412.7 1.8 collective-permute-start.14
  414.5 18.9 %mlp.6.refs_25_ = bf16[32,64,1024]{2,1,0:T(8,128)(2,1)} custom-call(bf16[8,64,256]{2,1,0:T(8,128)(2,1)S(1)} %get-tuple-element.37.refs_0_, bf16[8,64,256]{2,1,0:T(8,128)(2,1)} %collective-permute-done.27.refs_1_, bf16[8,64,256]{2,1,0:T(8,128)(2,1)} %collective-permute-done.28.refs_2_, ...), custom_call_target="tpu_custom_call", output_to_operand_aliasing={{}: (25, {})} | custom-call | flops 193273528320 | bytes 23068672 | tf_op jit(solution)/shard_map/mlp/pallas_call | solution.py:233
  433.4 19.0 %mlp.7 = bf16[32,64,1024]{2,1,0:T(8,128)(2,1)} custom-call(bf16[8,64,256]{2,1,0:T(8,128)(2,1)S(1)} %get-tuple-element.33.refs_0_, bf16[8,64,256]{2,1,0:T(8,128)(2,1)} %collective-permute-done.12.refs_1_, bf16[8,64,256]{2,1,0:T(8,128)(2,1)} %collective-permute-done.13.refs_2_, ...), custom_call_target="tpu_custom_call", output_to_operand_aliasing={{}: (25, {})} | custom-call | flops 193273528320 | bytes 23068672 | tf_op jit(solution)/shard_map/mlp/pallas_call | solution.py:233
  (69 shorter events, 0.2 us)
Async XLA Ops:
  3.2 30.2 %copy-start.6 = (bf16[1024]{0:T(1024)(128)(2,1)S(1)}, bf16[1024]{0:T(1024)(128)(2,1)}, u32[]{:S(2)}) copy-start(bf16[1024]{0:T(1024)(128)(2,1)} %param.29) | copy-start | bytes 6148
  3.2 51.9 %copy-start.18 = (s32[32]{0:T(128)S(1)}, s32[32]{0:T(128)}, u32[]{:S(2)}) copy-start(s32[32]{0:T(128)} %param.17) | copy-start | bytes 388
  3.2 52.0 %copy-start.4 = (bf16[1024,768]{1,0:T(8,128)(2,1)S(1)}, bf16[1024,768]{1,0:T(8,128)(2,1)}, u32[]{:S(2)}) copy-start(bf16[1024,768]{1,0:T(8,128)(2,1)} %param.22) | copy-start | bytes 4718596
  6.0 50.0 %copy-start.5 = (bf16[768]{0:T(1024)(128)(2,1)S(1)}, bf16[768]{0:T(1024)(128)(2,1)}, u32[]{:S(2)}) copy-start(bf16[768]{0:T(1024)(128)(2,1)} %param.23) | copy-start | bytes 4612
  6.0 50.1 %copy-start.7 = (bf16[1024]{0:T(1024)(128)(2,1)S(1)}, bf16[1024]{0:T(1024)(128)(2,1)}, u32[]{:S(2)}) copy-start(bf16[1024]{0:T(1024)(128)(2,1)} %param.25) | copy-start | bytes 6148
  6.0 50.2 %copy-start.8 = (bf16[1024]{0:T(1024)(128)(2,1)S(1)}, bf16[1024]{0:T(1024)(128)(2,1)}, u32[]{:S(2)}) copy-start(bf16[1024]{0:T(1024)(128)(2,1)} %param.26) | copy-start | bytes 6148
  6.0 50.2 %copy-start.9 = (bf16[1024]{0:T(1024)(128)(2,1)S(1)}, bf16[1024]{0:T(1024)(128)(2,1)}, u32[]{:S(2)}) copy-start(bf16[1024]{0:T(1024)(128)(2,1)} %param.27) | copy-start | bytes 6148
  6.0 50.2 %copy-start.10 = (bf16[1024]{0:T(1024)(128)(2,1)S(1)}, bf16[1024]{0:T(1024)(128)(2,1)}, u32[]{:S(2)}) copy-start(bf16[1024]{0:T(1024)(128)(2,1)} %param.31) | copy-start | bytes 6148
  6.0 27.4 %collective-permute-start.10 = (bf16[8,64,1024]{2,1,0:T(8,128)(2,1)}, bf16[8,64,1024]{2,1,0:T(8,128)(2,1)}, u32[]{:S(2)}, u32[]{:S(2)}) collective-permute-start(bf16[8,64,1024]{2,1,0:T(8,128)(2,1)} %ln1.7.a0), channel_id=1, source_target_pairs={{0,2},{2,0},{1,3},{3,1},{4,6},{6,4},{5,7},{7,5}} | collective-permute-start | bytes 3145736 | tf_op jit(solution)/shard_map/ppermute | solution.py:268
  12.0 50.2 %collective-permute-start.7 = (bf16[8,64,1024]{2,1,0:T(8,128)(2,1)}, bf16[8,64,1024]{2,1,0:T(8,128)(2,1)}, u32[]{:S(2)}, u32[]{:S(2)}) collective-permute-start(bf16[8,64,1024]{2,1,0:T(8,128)(2,1)} %ln1.6.a0), channel_id=1, source_target_pairs={{0,2},{2,0},{1,3},{3,1},{4,6},{6,4},{5,7},{7,5}} | collective-permute-start | bytes 3145736 | tf_op jit(solution)/shard_map/ppermute | solution.py:268
  12.0 51.9 %collective-permute-start.9 = (bf16[8,64,1024]{2,1,0:T(8,128)(2,1)}, bf16[8,64,1024]{2,1,0:T(8,128)(2,1)}, u32[]{:S(2)}, u32[]{:S(2)}) collective-permute-start(bf16[8,64,1024]{2,1,0:T(8,128)(2,1)} %ln1.7.a0), channel_id=1, source_target_pairs={{0,1},{1,0},{2,3},{3,2},{4,5},{5,4},{6,7},{7,6}} | collective-permute-start | bytes 3145736 | tf_op jit(solution)/shard_map/ppermute | solution.py:268
  33.4 30.8 %collective-permute-start.11 = (bf16[8,64,1024]{2,1,0:T(8,128)(2,1)}, bf16[8,64,1024]{2,1,0:T(8,128)(2,1)}, u32[]{:S(2)}, u32[]{:S(2)}) collective-permute-start(bf16[8,64,1024]{2,1,0:T(8,128)(2,1)} %collective-permute-done.10.a2), channel_id=1, source_target_pairs={{0,1},{1,0},{2,3},{3,2},{4,5},{5,4},{6,7},{7,6}} | collective-permute-start | bytes 3145736 | tf_op jit(solution)/shard_map/ppermute | solution.py:268
  33.4 28.2 %collective-permute-start.15 = (bf16[1,1024]{1,0:T(2,128)(2,1)S(1)}, bf16[1,1024]{1,0:T(2,128)(2,1)S(1)}, u32[]{:S(2)}, u32[]{:S(2)}) collective-permute-start(bf16[1,1024]{1,0:T(2,128)(2,1)S(1)} %reshape.45.refs_8_), channel_id=1, source_target_pairs={{0,1},{1,0},{2,3},{3,2},{4,5},{5,4},{6,7},{7,6}} | collective-permute-start | bytes 6152 | tf_op jit(solution)/shard_map/ppermute | solution.py:268
  33.9 21.2 %collective-permute-start.16 = (bf16[1,1024]{1,0:T(2,128)(2,1)S(1)}, bf16[1,1024]{1,0:T(2,128)(2,1)S(1)}, u32[]{:S(2)}, u32[]{:S(2)}) collective-permute-start(bf16[1,1024]{1,0:T(2,128)(2,1)S(1)} %reshape.45.refs_8_), channel_id=1, source_target_pairs={{0,2},{2,0},{1,3},{3,1},{4,6},{6,4},{5,7},{7,5}} | collective-permute-start | bytes 6152 | tf_op jit(solution)/shard_map/ppermute | solution.py:268
  55.1 7.1 %collective-permute-start.17 = (bf16[1,1024]{1,0:T(2,128)(2,1)S(1)}, bf16[1,1024]{1,0:T(2,128)(2,1)S(1)}, u32[]{:S(2)}, u32[]{:S(2)}) collective-permute-start(bf16[1,1024]{1,0:T(2,128)(2,1)S(1)} %collective-permute-done.16.refs_10_), channel_id=1, source_target_pairs={{0,1},{1,0},{2,3},{3,2},{4,5},{5,4},{6,7},{7,6}} | collective-permute-start | bytes 6152 | tf_op jit(solution)/shard_map/ppermute | solution.py:268
  56.2 5.4 %copy-start.1 = (bf16[8,64,1024]{2,1,0:T(8,128)(2,1)S(1)}, bf16[8,64,1024]{2,1,0:T(8,128)(2,1)}, u32[]{:S(2)}) copy-start(bf16[8,64,1024]{2,1,0:T(8,128)(2,1)} %ln1.6.a0) | copy-start | bytes 3145732
  61.6 75.4 %collective-permute-start.6 = (bf16[8,64,1024]{2,1,0:T(8,128)(2,1)S(1)}, bf16[8,64,1024]{2,1,0:T(8,128)(2,1)S(1)}, u32[]{:S(2)}, u32[]{:S(2)}) collective-permute-start(bf16[8,64,1024]{2,1,0:T(8,128)(2,1)S(1)} %copy-done.1), channel_id=1, source_target_pairs={{0,1},{1,0},{2,3},{3,2},{4,5},{5,4},{6,7},{7,6}} | collective-permute-start | bytes 3145736 | tf_op jit(solution)/shard_map/ppermute | solution.py:268
  62.1 72.6 %collective-permute-start.18 = (bf16[256,1024]{1,0:T(8,128)(2,1)}, bf16[256,1024]{1,0:T(8,128)(2,1)S(1)}, u32[]{:S(2)}, u32[]{:S(2)}) collective-permute-start(bf16[256,1024]{1,0:T(8,128)(2,1)} %refs_13_.7), channel_id=1, source_target_pairs={{0,1},{1,0},{2,3},{3,2},{4,5},{5,4},{6,7},{7,6}} | collective-permute-start | bytes 1572872 | tf_op jit(solution)/shard_map/ppermute | solution.py:268
  62.2 73.1 %collective-permute-start.19 = (bf16[256,1024]{1,0:T(8,128)(2,1)}, bf16[256,1024]{1,0:T(8,128)(2,1)}, u32[]{:S(2)}, u32[]{:S(2)}) collective-permute-start(bf16[256,1024]{1,0:T(8,128)(2,1)} %refs_13_.7), channel_id=1, source_target_pairs={{0,2},{2,0},{1,3},{3,1},{4,6},{6,4},{5,7},{7,5}} | collective-permute-start | bytes 1572872 | tf_op jit(solution)/shard_map/ppermute | solution.py:268
  63.9 73.1 %collective-permute-start.4 = (bf16[8,64,1024]{2,1,0:T(8,128)(2,1)}, bf16[8,64,1024]{2,1,0:T(8,128)(2,1)S(1)}, u32[]{:S(2)}, u32[]{:S(2)}) collective-permute-start(bf16[8,64,1024]{2,1,0:T(8,128)(2,1)} %ln1.5.a0), channel_id=1, source_target_pairs={{0,2},{2,0},{1,3},{3,1},{4,6},{6,4},{5,7},{7,5}} | collective-permute-start | bytes 3145736 | tf_op jit(solution)/shard_map/ppermute | solution.py:268
  64.2 73.3 %collective-permute-start.8 = (bf16[8,64,1024]{2,1,0:T(8,128)(2,1)}, bf16[8,64,1024]{2,1,0:T(8,128)(2,1)S(1)}, u32[]{:S(2)}, u32[]{:S(2)}) collective-permute-start(bf16[8,64,1024]{2,1,0:T(8,128)(2,1)} %collective-permute-done.7.a2), channel_id=1, source_target_pairs={{0,1},{1,0},{2,3},{3,2},{4,5},{5,4},{6,7},{7,6}} | collective-permute-start | bytes 3145736 | tf_op jit(solution)/shard_map/ppermute | solution.py:268
  64.2 70.6 %copy-start = (bf16[8,64,1024]{2,1,0:T(8,128)(2,1)S(1)}, bf16[8,64,1024]{2,1,0:T(8,128)(2,1)}, u32[]{:S(2)}) copy-start(bf16[8,64,1024]{2,1,0:T(8,128)(2,1)} %ln1.4.a0) | copy-start | bytes 3145732
  64.2 72.8 %copy-start.2 = (bf16[8,64,1024]{2,1,0:T(8,128)(2,1)S(1)}, bf16[8,64,1024]{2,1,0:T(8,128)(2,1)}, u32[]{:S(2)}) copy-start(bf16[8,64,1024]{2,1,0:T(8,128)(2,1)} %ln1.5.a0) | copy-start | bytes 3145732
  134.8 2.8 copy-start.16
  134.8 72.2 %collective-permute-start = (bf16[8,64,1024]{2,1,0:T(8,128)(2,1)S(1)}, bf16[8,64,1024]{2,1,0:T(8,128)(2,1)S(1)}, u32[]{:S(2)}, u32[]{:S(2)}) collective-permute-start(bf16[8,64,1024]{2,1,0:T(8,128)(2,1)S(1)} %copy-done), channel_id=1, source_target_pairs={{0,1},{1,0},{2,3},{3,2},{4,5},{5,4},{6,7},{7,6}} | collective-permute-start | bytes 3145736 | tf_op jit(solution)/shard_map/ppermute | solution.py:268
  135.3 72.2 %collective-permute-start.1 = (bf16[8,64,1024]{2,1,0:T(8,128)(2,1)S(1)}, bf16[8,64,1024]{2,1,0:T(8,128)(2,1)S(1)}, u32[]{:S(2)}, u32[]{:S(2)}) collective-permute-start(bf16[8,64,1024]{2,1,0:T(8,128)(2,1)S(1)} %copy-done), channel_id=1, source_target_pairs={{0,2},{2,0},{1,3},{3,1},{4,6},{6,4},{5,7},{7,5}} | collective-permute-start | bytes 3145736 | tf_op jit(solution)/shard_map/ppermute | solution.py:268
  137.1 70.8 %collective-permute-start.3 = (bf16[8,64,1024]{2,1,0:T(8,128)(2,1)S(1)}, bf16[8,64,1024]{2,1,0:T(8,128)(2,1)S(1)}, u32[]{:S(2)}, u32[]{:S(2)}) collective-permute-start(bf16[8,64,1024]{2,1,0:T(8,128)(2,1)S(1)} %copy-done.2), channel_id=1, source_target_pairs={{0,1},{1,0},{2,3},{3,2},{4,5},{5,4},{6,7},{7,6}} | collective-permute-start | bytes 3145736 | tf_op jit(solution)/shard_map/ppermute | solution.py:268
  137.1 70.8 %collective-permute-start.20 = (bf16[256,1024]{1,0:T(8,128)(2,1)}, bf16[256,1024]{1,0:T(8,128)(2,1)S(1)}, u32[]{:S(2)}, u32[]{:S(2)}) collective-permute-start(bf16[256,1024]{1,0:T(8,128)(2,1)} %collective-permute-done.19.refs_15_), channel_id=1, source_target_pairs={{0,1},{1,0},{2,3},{3,2},{4,5},{5,4},{6,7},{7,6}} | collective-permute-start | bytes 1572872 | tf_op jit(solution)/shard_map/ppermute | solution.py:268
  137.6 72.0 %collective-permute-start.5 = (bf16[8,64,1024]{2,1,0:T(8,128)(2,1)S(1)}, bf16[8,64,1024]{2,1,0:T(8,128)(2,1)S(1)}, u32[]{:S(2)}, u32[]{:S(2)}) collective-permute-start(bf16[8,64,1024]{2,1,0:T(8,128)(2,1)S(1)} %collective-permute-done.4.a2), channel_id=1, source_target_pairs={{0,1},{1,0},{2,3},{3,2},{4,5},{5,4},{6,7},{7,6}} | collective-permute-start | bytes 3145736 | tf_op jit(solution)/shard_map/ppermute | solution.py:268
  137.6 69.4 %copy-start.11 = (bf16[1024,1024]{1,0:T(8,128)(2,1)S(1)}, bf16[1024,1024]{1,0:T(8,128)(2,1)}, u32[]{:S(2)}) copy-start(bf16[1024,1024]{1,0:T(8,128)(2,1)} %refs_17_.7) | copy-start | bytes 6291460
  137.6 70.2 %copy-start.12 = (bf16[1024,1024]{1,0:T(8,128)(2,1)S(1)}, bf16[1024,1024]{1,0:T(8,128)(2,1)}, u32[]{:S(2)}) copy-start(bf16[1024,1024]{1,0:T(8,128)(2,1)} %refs_21_.7) | copy-start | bytes 6291460
  207.0 63.5 %collective-permute-start.21 = (bf16[1024,1024]{1,0:T(8,128)(2,1)S(1)}, bf16[1024,1024]{1,0:T(8,128)(2,1)S(1)}, u32[]{:S(2)}, u32[]{:S(2)}) collective-permute-start(bf16[1024,1024]{1,0:T(8,128)(2,1)S(1)} %copy-done.11), channel_id=1, source_target_pairs={{0,1},{1,0},{2,3},{3,2},{4,5},{5,4},{6,7},{7,6}} | collective-permute-start | bytes 6291464 | tf_op jit(solution)/shard_map/ppermute | solution.py:268
  207.5 63.8 %collective-permute-start.22 = (bf16[1024,1024]{1,0:T(8,128)(2,1)S(1)}, bf16[1024,1024]{1,0:T(8,128)(2,1)S(1)}, u32[]{:S(2)}, u32[]{:S(2)}) collective-permute-start(bf16[1024,1024]{1,0:T(8,128)(2,1)S(1)} %copy-done.11), channel_id=1, source_target_pairs={{0,2},{2,0},{1,3},{3,1},{4,6},{6,4},{5,7},{7,5}} | collective-permute-start | bytes 6291464 | tf_op jit(solution)/shard_map/ppermute | solution.py:268
  207.8 64.2 %collective-permute-start.24 = (bf16[1024,1024]{1,0:T(8,128)(2,1)S(1)}, bf16[1024,1024]{1,0:T(8,128)(2,1)}, u32[]{:S(2)}, u32[]{:S(2)}) collective-permute-start(bf16[1024,1024]{1,0:T(8,128)(2,1)S(1)} %copy-done.12), channel_id=1, source_target_pairs={{0,1},{1,0},{2,3},{3,2},{4,5},{5,4},{6,7},{7,6}} | collective-permute-start | bytes 6291464 | tf_op jit(solution)/shard_map/ppermute | solution.py:268
  207.8 1.9 copy-start.17
  207.9 93.1 %collective-permute-start.25 = (bf16[1024,1024]{1,0:T(8,128)(2,1)S(1)}, bf16[1024,1024]{1,0:T(8,128)(2,1)}, u32[]{:S(2)}, u32[]{:S(2)}) collective-permute-start(bf16[1024,1024]{1,0:T(8,128)(2,1)S(1)} %copy-done.12), channel_id=1, source_target_pairs={{0,2},{2,0},{1,3},{3,1},{4,6},{6,4},{5,7},{7,5}} | collective-permute-start | bytes 6291464 | tf_op jit(solution)/shard_map/ppermute | solution.py:268
  209.6 60.6 %collective-permute-start.2 = (bf16[8,64,1024]{2,1,0:T(8,128)(2,1)S(1)}, bf16[8,64,1024]{2,1,0:T(8,128)(2,1)S(1)}, u32[]{:S(2)}, u32[]{:S(2)}) collective-permute-start(bf16[8,64,1024]{2,1,0:T(8,128)(2,1)S(1)} %collective-permute-done.1.a2), channel_id=1, source_target_pairs={{0,1},{1,0},{2,3},{3,2},{4,5},{5,4},{6,7},{7,6}} | collective-permute-start | bytes 3145736 | tf_op jit(solution)/shard_map/ppermute | solution.py:268
  270.2 99.0 %collective-permute-start.33 = (bf16[8,64,256]{2,1,0:T(8,128)(2,1)S(1)}, bf16[8,64,256]{2,1,0:T(8,128)(2,1)S(1)}, u32[]{:S(2)}, u32[]{:S(2)}) collective-permute-start(bf16[8,64,256]{2,1,0:T(8,128)(2,1)S(1)} %get-tuple-element.46), channel_id=1, source_target_pairs={{0,1},{1,0},{2,3},{3,2},{4,5},{5,4},{6,7},{7,6}} | collective-permute-start | bytes 786440 | tf_op jit(solution)/shard_map/ppermute | solution.py:268
  270.5 98.7 %copy-start.13 = (bf16[1024,1024]{1,0:T(8,128)(2,1)}, bf16[1024,1024]{1,0:T(8,128)(2,1)S(1)}, u32[]{:S(2)}) copy-start(bf16[1024,1024]{1,0:T(8,128)(2,1)S(1)} %collective-permute-done.21.refs_18_) | copy-start | bytes 6291460
  270.5 99.2 %collective-permute-start.34 = (bf16[8,64,256]{2,1,0:T(8,128)(2,1)S(1)}, bf16[8,64,256]{2,1,0:T(8,128)(2,1)S(1)}, u32[]{:S(2)}, u32[]{:S(2)}) collective-permute-start(bf16[8,64,256]{2,1,0:T(8,128)(2,1)S(1)} %get-tuple-element.47), channel_id=1, source_target_pairs={{0,2},{2,0},{1,3},{3,1},{4,6},{6,4},{5,7},{7,5}} | collective-permute-start | bytes 786440 | tf_op jit(solution)/shard_map/ppermute | solution.py:268
  271.3 97.9 %copy-start.14 = (bf16[1024,1024]{1,0:T(8,128)(2,1)}, bf16[1024,1024]{1,0:T(8,128)(2,1)S(1)}, u32[]{:S(2)}) copy-start(bf16[1024,1024]{1,0:T(8,128)(2,1)S(1)} %collective-permute-done.22.refs_19_) | copy-start | bytes 6291460
  271.3 98.8 %collective-permute-start.35 = (bf16[8,64,256]{2,1,0:T(8,128)(2,1)S(1)}, bf16[8,64,256]{2,1,0:T(8,128)(2,1)S(1)}, u32[]{:S(2)}, u32[]{:S(2)}) collective-permute-start(bf16[8,64,256]{2,1,0:T(8,128)(2,1)S(1)} %get-tuple-element.48), channel_id=1, source_target_pairs={{0,3},{3,0},{1,2},{2,1},{4,7},{7,4},{5,6},{6,5}} | collective-permute-start | bytes 786440 | tf_op jit(solution)/shard_map/ppermute | solution.py:268
  272.1 98.0 %collective-permute-start.23 = (bf16[1024,1024]{1,0:T(8,128)(2,1)S(1)}, bf16[1024,1024]{1,0:T(8,128)(2,1)S(1)}, u32[]{:S(2)}, u32[]{:S(2)}) collective-permute-start(bf16[1024,1024]{1,0:T(8,128)(2,1)S(1)} %collective-permute-done.22.refs_19_), channel_id=1, source_target_pairs={{0,1},{1,0},{2,3},{3,2},{4,5},{5,4},{6,7},{7,6}} | collective-permute-start | bytes 6291464 | tf_op jit(solution)/shard_map/ppermute | solution.py:268
  300.9 72.3 %collective-permute-start.26 = (bf16[1024,1024]{1,0:T(8,128)(2,1)}, bf16[1024,1024]{1,0:T(8,128)(2,1)}, u32[]{:S(2)}, u32[]{:S(2)}) collective-permute-start(bf16[1024,1024]{1,0:T(8,128)(2,1)} %collective-permute-done.25.refs_23_), channel_id=1, source_target_pairs={{0,1},{1,0},{2,3},{3,2},{4,5},{5,4},{6,7},{7,6}} | collective-permute-start | bytes 6291464 | tf_op jit(solution)/shard_map/ppermute | solution.py:268
  301.0 72.4 %copy-start.3 = (bf16[256,1024]{1,0:T(8,128)(2,1)S(1)}, bf16[256,1024]{1,0:T(8,128)(2,1)}, u32[]{:S(2)}) copy-start(bf16[256,1024]{1,0:T(8,128)(2,1)} %refs_13_.7) | copy-start | bytes 1572868
  369.2 64.1 %collective-permute-start.12 = (bf16[8,64,256]{2,1,0:T(8,128)(2,1)}, bf16[8,64,256]{2,1,0:T(8,128)(2,1)}, u32[]{:S(2)}, u32[]{:S(2)}) collective-permute-start(bf16[8,64,256]{2,1,0:T(8,128)(2,1)} %get-tuple-element.34), channel_id=1, source_target_pairs={{0,1},{1,0},{2,3},{3,2},{4,5},{5,4},{6,7},{7,6}} | collective-permute-start | bytes 786440 | tf_op jit(solution)/shard_map/ppermute | solution.py:268
  369.8 63.6 %collective-permute-start.13 = (bf16[8,64,256]{2,1,0:T(8,128)(2,1)}, bf16[8,64,256]{2,1,0:T(8,128)(2,1)}, u32[]{:S(2)}, u32[]{:S(2)}) collective-permute-start(bf16[8,64,256]{2,1,0:T(8,128)(2,1)} %get-tuple-element.35), channel_id=1, source_target_pairs={{0,2},{2,0},{1,3},{3,1},{4,6},{6,4},{5,7},{7,5}} | collective-permute-start | bytes 786440 | tf_op jit(solution)/shard_map/ppermute | solution.py:268
  370.1 21.7 %collective-permute-start.30 = (bf16[8,64,256]{2,1,0:T(8,128)(2,1)}, bf16[8,64,256]{2,1,0:T(8,128)(2,1)}, u32[]{:S(2)}, u32[]{:S(2)}) collective-permute-start(bf16[8,64,256]{2,1,0:T(8,128)(2,1)} %get-tuple-element.42), channel_id=1, source_target_pairs={{0,1},{1,0},{2,3},{3,2},{4,5},{5,4},{6,7},{7,6}} | collective-permute-start | bytes 786440 | tf_op jit(solution)/shard_map/ppermute | solution.py:268
  370.1 1.4 copy-start.15
  371.5 20.6 %collective-permute-start.31 = (bf16[8,64,256]{2,1,0:T(8,128)(2,1)}, bf16[8,64,256]{2,1,0:T(8,128)(2,1)}, u32[]{:S(2)}, u32[]{:S(2)}) collective-permute-start(bf16[8,64,256]{2,1,0:T(8,128)(2,1)} %get-tuple-element.43), channel_id=1, source_target_pairs={{0,2},{2,0},{1,3},{3,1},{4,6},{6,4},{5,7},{7,5}} | collective-permute-start | bytes 786440 | tf_op jit(solution)/shard_map/ppermute | solution.py:268
  373.2 20.6 %collective-permute-start.32 = (bf16[8,64,256]{2,1,0:T(8,128)(2,1)}, bf16[8,64,256]{2,1,0:T(8,128)(2,1)}, u32[]{:S(2)}, u32[]{:S(2)}) collective-permute-start(bf16[8,64,256]{2,1,0:T(8,128)(2,1)} %get-tuple-element.44), channel_id=1, source_target_pairs={{0,3},{3,0},{1,2},{2,1},{4,7},{7,4},{5,6},{6,5}} | collective-permute-start | bytes 786440 | tf_op jit(solution)/shard_map/ppermute | solution.py:268
  391.8 20.9 %collective-permute-start.27 = (bf16[8,64,256]{2,1,0:T(8,128)(2,1)}, bf16[8,64,256]{2,1,0:T(8,128)(2,1)}, u32[]{:S(2)}, u32[]{:S(2)}) collective-permute-start(bf16[8,64,256]{2,1,0:T(8,128)(2,1)} %get-tuple-element.38), channel_id=1, source_target_pairs={{0,1},{1,0},{2,3},{3,2},{4,5},{5,4},{6,7},{7,6}} | collective-permute-start | bytes 786440 | tf_op jit(solution)/shard_map/ppermute | solution.py:268
  392.1 22.3 %collective-permute-start.28 = (bf16[8,64,256]{2,1,0:T(8,128)(2,1)}, bf16[8,64,256]{2,1,0:T(8,128)(2,1)}, u32[]{:S(2)}, u32[]{:S(2)}) collective-permute-start(bf16[8,64,256]{2,1,0:T(8,128)(2,1)} %get-tuple-element.39), channel_id=1, source_target_pairs={{0,2},{2,0},{1,3},{3,1},{4,6},{6,4},{5,7},{7,5}} | collective-permute-start | bytes 786440 | tf_op jit(solution)/shard_map/ppermute | solution.py:268
  393.8 20.6 %collective-permute-start.29 = (bf16[8,64,256]{2,1,0:T(8,128)(2,1)}, bf16[8,64,256]{2,1,0:T(8,128)(2,1)}, u32[]{:S(2)}, u32[]{:S(2)}) collective-permute-start(bf16[8,64,256]{2,1,0:T(8,128)(2,1)} %get-tuple-element.40), channel_id=1, source_target_pairs={{0,3},{3,0},{1,2},{2,1},{4,7},{7,4},{5,6},{6,5}} | collective-permute-start | bytes 786440 | tf_op jit(solution)/shard_map/ppermute | solution.py:268
  412.7 20.7 %collective-permute-start.14 = (bf16[8,64,256]{2,1,0:T(8,128)(2,1)}, bf16[8,64,256]{2,1,0:T(8,128)(2,1)}, u32[]{:S(2)}, u32[]{:S(2)}) collective-permute-start(bf16[8,64,256]{2,1,0:T(8,128)(2,1)} %get-tuple-element.36), channel_id=1, source_target_pairs={{0,3},{3,0},{1,2},{2,1},{4,7},{7,4},{5,6},{6,5}} | collective-permute-start | bytes 786440 | tf_op jit(solution)/shard_map/ppermute | solution.py:268

commit v2 on v1

v2 whole, which is shorter than its diff:
```python
import functools

import jax
import jax.numpy as jnp
from jax import lax
from jax.experimental import pallas as pl
from jax.experimental.pallas import tpu as pltpu
from jax.sharding import PartitionSpec as P


LN_EPS = 1e-5
LOG2E = 1.4426950408889634
NEG = -1e30
CHUNKS = (4, 4, 8, 8, 8)
GROUPS = ((0, 1), (2,), (3,), (4,))
KB = 256
XOR1 = [(0, 1), (1, 0), (2, 3), (3, 2)]
XOR2 = [(0, 2), (2, 0), (1, 3), (3, 1)]
XOR3 = [(0, 3), (3, 0), (1, 2), (2, 1)]


def norm_rows(rows_f32, gain, bias):
    row_mean = jnp.mean(rows_f32, axis=-1, keepdims=True)
    centered = rows_f32 - row_mean
    row_var = jnp.mean(centered * centered, axis=-1, keepdims=True)
    normed = centered * lax.rsqrt(row_var + LN_EPS)
    return (normed * gain + bias).astype(jnp.bfloat16)


def ln_kernel(x_ref, gain_ref, bias_ref, o_ref):
    rows = x_ref[...].reshape(-1, x_ref.shape[-1]).astype(jnp.float32)
    gain = gain_ref[...].astype(jnp.float32)
    bias = bias_ref[...].astype(jnp.float32)
    o_ref[...] = norm_rows(rows, gain, bias).reshape(o_ref.shape)


def layer_norm_chunk(x, gain, bias, start, count):
    tok, dim = x.shape[1], x.shape[2]
    step = 4
    return pl.pallas_call(
        ln_kernel,
        grid=(count // step,),
        in_specs=[
            pl.BlockSpec((step, tok, dim), lambda i: (start // step + i, 0, 0)),
            pl.BlockSpec((1, dim), lambda i: (0, 0)),
            pl.BlockSpec((1, dim), lambda i: (0, 0)),
        ],
        out_specs=pl.BlockSpec((step, tok, dim), lambda i: (i, 0, 0)),
        out_shape=jax.ShapeDtypeStruct((count, tok, dim), jnp.bfloat16),
        cost_estimate=pl.CostEstimate(flops=count * tok * dim * 10, bytes_accessed=count * tok * dim * 4, transcendentals=0),
        name='ln1',
    )(x, gain, bias)


def attn_kernel(start, meta_ref, slope_ref, a0, a1, a2, a3, w_ref, b_ref, kc_ref, vc_ref, *rest):
    has_prev = start > 0
    if has_prev:
        rest = rest[2:]
    c0, c1, c2, c3, ko_ref, vo_ref, a_scr, qkv_scr, bias_scr, m_scr, acc_scr, ctx_scr, s_scr, top_scr = rest
    heads, hd, cache_len = kc_ref.shape[1:]
    tok = a0.shape[1]
    chunk = 4 * tok
    tp = meta_ref[0]
    step = pl.program_id(0)
    pos = meta_ref[1 + start + step]

    diff = (lax.broadcasted_iota(jnp.int32, (KB, chunk), 0) - lax.broadcasted_iota(jnp.int32, (KB, chunk), 1))

    @pl.when(step == 0)
    def _():
        for h in range(heads):
            bias_scr[h] = diff.astype(jnp.float32) * (slope_ref[h] * LOG2E)

    for k, blk in enumerate((a0, a1, a2, a3)):
        a_scr[pl.ds(pl.multiple_of((tp ^ k) * tok, tok), tok), :] = blk[0]
    qkv = lax.dot_general(w_ref[...], a_scr[...], (((1,), (1,)), ((), ())), preferred_element_type=jnp.float32)
    qkv = qkv + b_ref[...]
    qkv_scr[...] = qkv.astype(jnp.bfloat16)

    ko_ref[...] = kc_ref[...]
    vo_ref[...] = vc_ref[...]
    win = chunk + 128
    base = pl.multiple_of(jnp.minimum((pos // 128) * 128, cache_len - win), 128)
    off = pos - base
    lane = lax.broadcasted_iota(jnp.int32, (hd, win), 1)
    inside = (lane >= off) & (lane < off + chunk)
    pad = jnp.zeros((hd, 128), jnp.float32)
    for h in range(heads):
        for part, dst in ((1, ko_ref), (2, vo_ref)):
            row = h * 3 * hd + part * hd
            new = qkv_scr[row:row + hd, :].astype(jnp.float32)
            new = pltpu.roll(jnp.concatenate([new, pad], axis=1), off, 1)
            old = dst[0, h, :, pl.ds(base, win)].astype(jnp.float32)
            dst[0, h, :, pl.ds(base, win)] = jnp.where(inside, new, old).astype(jnp.bfloat16)

    m_scr[...] = jnp.full_like(m_scr, NEG)
    acc_scr[...] = jnp.zeros_like(acc_scr)
    ones = jnp.ones((16, KB), jnp.bfloat16)

    def raw_scores(h, kb):
        keys = ko_ref[0, h, :, pl.ds(pl.multiple_of(kb * KB, KB), KB)]
        q = qkv_scr[h * 3 * hd:h * 3 * hd + hd, :]
        return lax.dot_general(keys, q, (((0,), (0,)), ((), ())), preferred_element_type=jnp.float32)

    def keep_scores(h, kb, s, masked):
        bias = bias_scr[h]
        s = s * (LOG2E * hd ** -0.5) + bias
        if masked:
            bound = (pos - kb * KB).astype(jnp.float32) * (slope_ref[h] * LOG2E)
            s = jnp.where(bias <= bound, s, NEG)
        s_scr[h] = s
        top_scr[h] = jnp.max(s, axis=0, keepdims=True)

    def weigh(h, kb):
        j0 = pl.multiple_of(kb * KB, KB)
        vals = jnp.concatenate([vo_ref[0, h, :, pl.ds(j0, KB)], ones], axis=0)
        shift = slope_ref[h] * LOG2E * (j0 - pos).astype(jnp.float32)
        m_old = m_scr[h]
        m_new = jnp.maximum(m_old, top_scr[h] + shift)
        p = jnp.exp2(s_scr[h] - (m_new - shift)).astype(jnp.bfloat16)
        alpha = jnp.exp2(m_old - m_new)
        m_scr[h] = m_new
        acc_scr[h] = acc_scr[h] * alpha + jnp.dot(vals, p, preferred_element_type=jnp.float32)

    def both(kb, masked):
        for h in range(heads):
            s = raw_scores(h, kb + 1)
            weigh(h, kb)
            keep_scores(h, kb + 1, s, masked)

    full = pos // KB
    total = (pos + chunk + KB - 1) // KB
    first = [raw_scores(h, 0) for h in range(heads)]
    for h in range(heads):
        keep_scores(h, 0, first[h], True)
    split = jnp.maximum(full - 1, 0)
    lax.fori_loop(0, split, lambda kb, c: (both(kb, False), c)[1], 0)
    lax.fori_loop(split, total - 1, lambda kb, c: (both(kb, True), c)[1], 0)
    for h in range(heads):
        weigh(h, total - 1)

    for h in range(heads):
        ctx = acc_scr[h, :hd, :] / acc_scr[h, hd:hd + 1, :]
        ctx_scr[:, h * hd:(h + 1) * hd] = ctx.T.astype(jnp.bfloat16)
    for k, out in enumerate((c0, c1, c2, c3)):
        out[0] = ctx_scr[pl.ds(pl.multiple_of((tp ^ k) * tok, tok), tok), :]


def attention_chunk(meta, slopes, blocks, w_t, b_col, k_t, v_t, prev, start):
    count, tok, dim = blocks[0].shape
    heads, hd, cache_len = k_t.shape[1:]
    chunk = 4 * tok
    cols = heads * hd
    tok_spec = pl.BlockSpec((1, tok, dim), lambda i, *_: (i, 0, 0))
    cache_spec = pl.BlockSpec((1, heads, hd, cache_len), lambda i, *_: (start + i, 0, 0, 0))
    any_spec = pl.BlockSpec(memory_space=pl.ANY)
    in_specs = [tok_spec] * 4 + [
        pl.BlockSpec(w_t.shape, lambda i, *_: (0, 0)),
        pl.BlockSpec(b_col.shape, lambda i, *_: (0, 0)),
        cache_spec, cache_spec]
    operands = [*blocks, w_t, b_col, k_t, v_t]
    aliases = {}
    if prev is not None:
        in_specs += [any_spec, any_spec]
        operands += list(prev)
        aliases = {2 + 8: 4, 2 + 9: 5}
    ctx_spec = pl.BlockSpec((1, tok, cols), lambda i, *_: (i, 0, 0))
    return pl.pallas_call(
        functools.partial(attn_kernel, start),
        grid_spec=pltpu.PrefetchScalarGridSpec(
            num_scalar_prefetch=2,
            grid=(count,),
            in_specs=in_specs,
            out_specs=[ctx_spec] * 4 + [cache_spec, cache_spec],
            scratch_shapes=[
                pltpu.VMEM((chunk, dim), jnp.bfloat16),
                pltpu.VMEM((3 * cols, chunk), jnp.bfloat16),
                pltpu.VMEM((heads, KB, chunk), jnp.float32),
                pltpu.VMEM((heads, 1, chunk), jnp.float32),
                pltpu.VMEM((heads, hd + 16, chunk), jnp.float32),
                pltpu.VMEM((chunk, cols), jnp.bfloat16),
                pltpu.VMEM((heads, KB, chunk), jnp.float32),
                pltpu.VMEM((heads, 1, chunk), jnp.float32),
            ]),
        out_shape=[jax.ShapeDtypeStruct((count, tok, cols), jnp.bfloat16)] * 4
        + [jax.ShapeDtypeStruct(k_t.shape, k_t.dtype)] * 2,
        input_output_aliases=aliases,
        cost_estimate=pl.CostEstimate(
            flops=count * 3_000_000_000, bytes_accessed=count * 4 * heads * hd * cache_len * 2, transcendentals=0),
        compiler_params=pltpu.CompilerParams(vmem_limit_bytes=40 * 1024 * 1024),
        name='attn',
    )(meta, slopes, *operands)


def mlp_kernel(nsub, half_ref, *refs):
    ctx_refs = refs[:4 * nsub]
    x_ref, bo_ref, g2_ref, b2_ref, bd_ref = refs[4 * nsub:4 * nsub + 5]
    packs = refs[4 * nsub + 5:4 * nsub + 17]
    o_ref, wu, wd, wo, bu, ctx_scr, n_scr, r_scr, h_scr, y_scr, sem_a, sem_b, sem_o, sem_u = refs[-14:]
    rows, dim = n_scr.shape
    hid = wd.shape[1]
    tok = x_ref.shape[1]
    cut = wo.shape[0] // 8

    def copies(j):
        pa, pb = (packs[0].at[j], packs[1].at[j]) if j < 2 else (packs[2].at[j - 2], packs[3].at[j - 2]) if j < 4 else (packs[2 * j - 4], packs[2 * j - 3])
        return (pltpu.make_async_copy(pa.at[pl.ds(hid, cut), :], wo.at[pl.ds(j * cut, cut), :], sem_o.at[j]),
                pltpu.make_async_copy(pa.at[pl.ds(hid + cut, 16), :], bu.at[j], sem_u.at[j]),
                pltpu.make_async_copy(pa.at[pl.ds(0, hid), :], wu.at[j], sem_a.at[j]),
                pltpu.make_async_copy(pb, wd.at[j], sem_b.at[j]))

    for part in (0, 1):
        for j in range(8):
            copies(j)[part].start()
    for j in range(8):
        copies(j)[2].start()
        copies(j)[3].start()

    half = half_ref[0]
    for i in range(nsub):
        size = ctx_refs[4 * i].shape[0] * tok
        for k in range(4):
            for side in (0, 1):
                pick = half if side == 0 else 1 - half
                at = side * cut if k < 2 else pl.multiple_of(pick * cut, cut)
                piece = ctx_refs[4 * i + k][:, :, pl.ds(at, cut)].reshape(size, cut)
                ctx_scr[i * size:(i + 1) * size, (2 * k + side) * cut:(2 * k + side + 1) * cut] = piece
    for j in range(8):
        copies(j)[0].wait()
        copies(j)[1].wait()

    y = jnp.dot(ctx_scr[...], wo[...], preferred_element_type=jnp.float32)
    r = (x_ref[...].reshape(rows, dim).astype(jnp.float32) + y + bo_ref[...].astype(jnp.float32)).astype(jnp.bfloat16)
    r_scr[...] = r
    n_scr[...] = norm_rows(r.astype(jnp.float32), g2_ref[...].astype(jnp.float32), b2_ref[...].astype(jnp.float32))
    y_scr[...] = jnp.zeros_like(y_scr)
    lim = 256

    def wait_pack(j):
        pltpu.make_async_copy(packs[1].at[0], wu.at[j], sem_a.at[j]).wait()
        pltpu.make_async_copy(packs[1].at[0], wd.at[j], sem_b.at[j]).wait()

    def up(m, j):
        return (jnp.dot(n_scr[m:m + lim, :hid], wu[j, :, :hid], preferred_element_type=jnp.float32)
                + jnp.dot(n_scr[m:m + lim, hid:], wu[j, :, hid:], preferred_element_type=jnp.float32))

    def act(m, j, pre):
        h_scr[m:m + lim, :] = jax.nn.gelu(pre + bu[j, 0:1, :hid].astype(jnp.float32), approximate=True).astype(jnp.bfloat16)

    def down(m, j):
        y_scr[m:m + lim, :] += jnp.dot(h_scr[m:m + lim, :], wd[j], preferred_element_type=jnp.float32)

    steps = range(0, rows, lim)
    wait_pack(0)
    pre = [up(m, 0) for m in steps]
    for m, p in zip(steps, pre):
        act(m, 0, p)

    def body(j, c):
        wait_pack(j + 1)
        pre = [up(m, j + 1) for m in steps]
        for m, p in zip(steps, pre):
            down(m, j)
            act(m, j + 1, p)
        return c

    lax.fori_loop(0, 7, body, 0)
    for m in steps:
        down(m, 7)
    out = r_scr[...].astype(jnp.float32) + y_scr[...] + bd_ref[...].astype(jnp.float32)
    o_ref[...] = out.astype(jnp.bfloat16).reshape(o_ref.shape)


def mlp_chunk(half, ctx, x, small, packs, prev, start, count):
    tok, cols = ctx[0].shape[1:]
    dim = x.shape[2]
    rows = count * tok
    hid = packs[1].shape[1]
    whole = lambda a: pl.BlockSpec(a.shape, lambda i, *_: (0,) * a.ndim)
    any_spec = pl.BlockSpec(memory_space=pl.ANY)
    x_spec = pl.BlockSpec((count, tok, dim), lambda i, *_: (start // count, 0, 0))
    in_specs = [whole(c) for c in ctx] + [x_spec] + [whole(a) for a in small] + [any_spec] * 12
    operands = [half, *ctx, x, *small, *packs]
    aliases = {}
    if prev is not None:
        aliases = {len(operands): 0}
        in_specs.append(any_spec)
        operands.append(prev)
    return pl.pallas_call(
        functools.partial(mlp_kernel, len(ctx) // 4),
        grid_spec=pltpu.PrefetchScalarGridSpec(
            num_scalar_prefetch=1,
            grid=(1,),
            in_specs=in_specs,
            out_specs=x_spec,
            scratch_shapes=[
                pltpu.VMEM((8, hid, dim), jnp.bfloat16),
                pltpu.VMEM((8, hid, dim), jnp.bfloat16),
                pltpu.VMEM((4 * cols, dim), jnp.bfloat16),
                pltpu.VMEM((8, 16, dim), jnp.bfloat16),
                pltpu.VMEM((rows, 4 * cols), jnp.bfloat16),
                pltpu.VMEM((rows, dim), jnp.bfloat16),
                pltpu.VMEM((rows, dim), jnp.bfloat16),
                pltpu.VMEM((rows, hid), jnp.bfloat16),
                pltpu.VMEM((rows, dim), jnp.float32),
                pltpu.SemaphoreType.DMA((8,)),
                pltpu.SemaphoreType.DMA((8,)),
                pltpu.SemaphoreType.DMA((8,)),
                pltpu.SemaphoreType.DMA((8,)),
            ]),
        out_shape=jax.ShapeDtypeStruct(x.shape, x.dtype),
        input_output_aliases=aliases,
        cost_estimate=pl.CostEstimate(
            flops=rows * 9 * dim * dim * 2, bytes_accessed=rows * dim * 8 + 18 * dim * dim, transcendentals=0),
        compiler_params=pltpu.CompilerParams(vmem_limit_bytes=52 * 1024 * 1024),
        name='mlp',
    )(*operands)


def solution(mesh):
    tp_size = mesh.shape['tp']

    def local_layer(x, prefix_len, k_cache, v_cache, ln1_gain, ln1_bias, w_qkv, b_qkv, w_out, b_out, ln2_gain, ln2_bias, w_up, b_up, w_down, b_down):
        heads = k_cache.shape[2]
        dim = x.shape[2]
        tp = lax.axis_index('tp')
        dp = lax.axis_index('dp')
        row = lambda a: a.reshape(1, -1)

        def perm(a, pairs, axis='tp'):
            return lax.ppermute(a, axis, pairs)

        def gather(a):
            far = perm(a, XOR2)
            return [a, perm(a, XOR1), far, perm(far, XOR1)]

        starts = [sum(CHUNKS[:c]) for c in range(len(CHUNKS))]
        normed = []
        for c, s in enumerate(starts):
            normed.append(layer_norm_chunk(x, row(ln1_gain), row(ln1_bias), s, CHUNKS[c]))
        blocks = [gather(n) for n in normed]

        half = w_up.shape[1] // 2
        cut = w_out.shape[0] // 2
        pad = jnp.zeros((15, dim), jnp.bfloat16)
        pack_a, pack_b = [], []
        for i in range(2):
            up = w_up[:, i * half:(i + 1) * half]
            bias = jnp.concatenate([row(b_up)[:, i * half:(i + 1) * half], pad[:1, :dim - half]], axis=1)
            pack_a.append(jnp.concatenate([
                jnp.concatenate([up[:half], up[half:]], axis=1), w_out[i * cut:(i + 1) * cut], bias, pad], axis=0))
            pack_b.append(w_down[i * half:(i + 1) * half])
        pack_a, pack_b = jnp.stack(pack_a), jnp.stack(pack_b)
        packs = [pack_a, pack_b, perm(pack_a, XOR1), perm(pack_b, XOR1)]
        far = []
        for pack in (pack_a, pack_b):
            mine = lax.dynamic_index_in_dim(pack, dp, 0, keepdims=False)
            direct = perm(mine, XOR2)
            side = perm(direct, [(0, 1), (1, 0)], 'dp')
            far.append((direct, side, perm(direct, XOR1), perm(side, XOR1)))
        for k in range(4):
            packs += [far[0][k], far[1][k]]

        meta = jnp.concatenate([tp[None].astype(jnp.int32), prefix_len])
        head_ids = tp * heads + jnp.arange(heads)
        slopes = jnp.exp2(-8.0 * (head_ids + 1).astype(jnp.float32) / (heads * tp_size))
        w_t = w_qkv.T
        b_col = b_qkv.astype(jnp.float32).reshape(-1, 1)
        k_t = k_cache.transpose(0, 2, 3, 1)
        v_t = v_cache.transpose(0, 2, 3, 1)
        small = [row(b_out), row(ln2_gain), row(ln2_bias), row(b_down)]
        my_half = dp[None].astype(jnp.int32)

        caches, x_out = None, None
        sent = []
        for c, s in enumerate(starts):
            outs = attention_chunk(meta, slopes, blocks[c], w_t, b_col, k_t, v_t, caches, s)
            caches = outs[4:]
            sent.append([outs[0], perm(outs[1], XOR1), perm(outs[2], XOR2), perm(outs[3], XOR3)])
        for g in GROUPS:
            s, n = starts[g[0]], sum(CHUNKS[c] for c in g)
            ctx = sum((sent[c] for c in g), [])
            x_out = mlp_chunk(my_half, ctx, x, small, packs, x_out, s, n)
        return x_out, caches[0].transpose(0, 3, 1, 2), caches[1].transpose(0, 3, 1, 2)

    tok_spec = P('dp', 'tp', None)
    cache_spec = P('dp', None, 'tp', None)
    replicated = P()
    in_specs = (tok_spec, P('dp'), cache_spec, cache_spec, replicated, replicated, P(None, 'tp'), P('tp'), P('tp', None), replicated, replicated, replicated, P(None, 'tp'), P('tp'), P('tp', None), replicated)

    return jax.shard_map(local_layer, mesh=mesh, in_specs=in_specs, out_specs=(tok_spec, cache_spec, cache_spec), check_vma=False)
```

time: 448 us -> 380 us (0.85); the launches traced: 453 us -> 372 us
  Pallas kernels: 354 us -> 246 us
  local copies, waits for them, and re-layouts: 4.97 us -> 18.1 us
  other arithmetic: 0.08 us -> 8.55 us
  starting transfers between devices: 23 us -> 28.3 us
    pallas_call x4 -> x5, Pallas kernels: 269 us -> 139 us  [attention_chunk(): pl.pallas_call(functools.partial(attn_kernel, start), grid_spec=pltpu.Pre...]
    pallas_call x4, Pallas kernels: 75.1 us -> 94.1 us  [mlp_chunk(): pl.pallas_call(functools.partial(mlp_kernel, len(ctx) // 4), grid_spec=pl...]
    ppermute x36 -> x40, starting transfers between devices: 23 us -> 28.3 us  [perm(): return lax.ppermute(a, axis, pairs)]
    unnamed x39 -> x69, local copies, waits for them, and re-layouts: 2.23 us -> 7.26 us
    another operation x0 -> x3, other arithmetic: none -> 4.91 us  [local_layer(): pack_a, pack_b = (jnp.stack(pack_a), jnp.stack(pack_b))]
    pallas_call x4 -> x5, Pallas kernels: 10.8 us -> 12.5 us  [layer_norm_chunk(): pl.pallas_call(ln_kernel, grid=(count // step,), in_specs=[pl.BlockSpec((...]
    ppermute x36 -> x40, waiting for transfers between devices: 68.8 us -> 70 us  [perm(): return lax.ppermute(a, axis, pairs)]
  transfers between devices with their start and end apart: 36 -> 40, of which waited for: 3 -> 7; matrix products, arithmetic and copies ran while one was open for 0% -> 5% of each run, Pallas kernels for 73% -> 59%
where the time goes in v2:
time: 380 us; the launch traced here: 372 us
  Pallas kernels  246 us (65%)
  waiting for transfers between devices  70 us (18%)
  starting transfers between devices  28.3 us (7%)
  local copies, waits for them, and re-layouts  18.1 us (5%)
  other arithmetic  8.55 us (2%)
    pallas_call x5, Pallas kernels, attention_chunk(): pl.pallas_call(functools.partial(attn_kernel, start), grid_spec=pltpu.Pre...  139 us
    pallas_call x4, Pallas kernels, mlp_chunk(): pl.pallas_call(functools.partial(mlp_kernel, len(ctx) // 4), grid_spec=pl...  94.1 us
    ppermute x40, waiting for transfers between devices, perm(): return lax.ppermute(a, axis, pairs)  70 us
    ppermute x40, starting transfers between devices, perm(): return lax.ppermute(a, axis, pairs)  28.3 us
    pallas_call x5, Pallas kernels, layer_norm_chunk(): pl.pallas_call(ln_kernel, grid=(count // step,), in_specs=[pl.BlockSpec((...  12.5 us
  transfers between devices with their start and end apart: 40, of which 7 were waited for; matrix products, arithmetic and copies ran while one was open for 5% of the time, Pallas kernels for 59%

profile of v2, /device:TPU:0, one launch (start us, length us, event | category | flops | bytes accessed | tf_op | source)
XLA Modules:
  0.0 372.1 jit_solution(2748911977808364115)
XLA Ops:
  0.6 1.3 reshape.43.gain_ref
  1.9 1.3 reshape.44.bias_ref
  3.2 2.7 ln1.5.a0
  5.8 0.8 collective-permute-start
  6.7 2.5 collective-permute-start.1
  9.1 2.3 ln1.8.a0
  11.6 0.3 collective-permute-start.10
  11.9 2.2 ln1.9.a0
  14.1 1.7 collective-permute-start.13
  15.9 0.8 fusion.10
  16.6 2.9 fusion.9
  19.5 1.2 slice_bitcast_fusion.1
  20.8 1.6 fusion.8
  22.6 0.3 copy-done.19
  23.0 4.5 %maximum_bitcast_fusion = (bf16[1,656,1024]{2,1,0:T(8,128)(2,1)}, bf16[1,656,1024]{2,1,0:T(8,128)(2,1)}) fusion(bf16[1,1024]{1,0:T(2,128)(2,1)S(1)} %concatenate.26, bf16[128,1024]{1,0:T(8,128)(2,1)S(1)} %get-tuple-element.69, bf16[512,512]{1,0:T(8,128)(2,1)S(1)} %copy-done.18, bf16[512,512]{1,0:T(8,128)(2,1)S(1)} %copy-done.17, ...), kind=kLoop, calls=%fused_computation.15 | loop fusion | flops 15450112 | bytes 5312800 | tf_op jit(solution)/shard_map/stack | solution.py:353
  27.5 0.8 copy-done.5
  28.3 27.5 %collective-permute-done.13.a2 = bf16[4,64,1024]{2,1,0:T(8,128)(2,1)} collective-permute-done((bf16[4,64,1024]{2,1,0:T(8,128)(2,1)}, bf16[4,64,1024]{2,1,0:T(8,128)(2,1)}, u32[]{:S(2)}, u32[]{:S(2)}) %collective-permute-start.13) | collective-permute-done | bytes 524320 | tf_op jit(solution)/shard_map/ppermute | solution.py:331
  55.8 1.7 copy.31
  57.7 0.7 reshape.48.refs_10_.refs_6_
  58.4 1.3 reshape.49.refs_11_.refs_7_
  59.7 1.3 reshape.50.refs_12_.refs_8_
  61.0 2.6 ln1.6.a0
  63.6 2.7 ln1.7.a0
  66.3 2.0 fusion.6
  68.5 1.1 copy-done.9
  69.6 0.4 copy-done.10
  70.0 0.2 pad_maximum_fusion.refs_13_.refs_9_
  70.3 1.7 copy-done.1
  72.0 0.5 collective-permute-start.3
  72.5 1.7 collective-permute-start.4
  74.3 1.1 collective-permute-start.7
  75.4 19.6 %attn.5 = (bf16[4,64,256]{2,1,0:T(8,128)(2,1)S(1)}, bf16[4,64,256]{2,1,0:T(8,128)(2,1)S(1)}, bf16[4,64,256]{2,1,0:T(8,128)(2,1)S(1)}, bf16[4,64,256]{2,1,0:T(8,1...) custom-call(s32[33]{0:T(128)S(1)} %pad_add_fusion.meta_ref, ...), custom_call_target="tpu_custom_call" | custom-call | flops 12000000000 | bytes 16777216 | tf_op jit(solution)/shard_map/attn/pallas_call | solution.py:168
  95.0 1.2 collective-permute-start.21
  96.2 2.4 collective-permute-done.4.a2
  98.6 1.7 collective-permute-start.35
  100.3 20.7 %collective-permute-done.7.a2 = bf16[8,64,1024]{2,1,0:T(8,128)(2,1)S(1)} collective-permute-done((bf16[8,64,1024]{2,1,0:T(8,128)(2,1)S(1)}, bf16[8,64,1024]{2,1,0:T(8,128)(2,1)S(1)}, u32[]{:S(2)}, u32[]{:S(2)}) %collective-permute-start.7) | collective-permute-done | bytes 1048608 | tf_op jit(solution)/shard_map/ppermute | solution.py:331
  121.1 1.9 collective-permute-start.8
  122.9 19.8 %attn.6 = (bf16[4,64,256]{2,1,0:T(8,128)(2,1)S(1)}, bf16[4,64,256]{2,1,0:T(8,128)(2,1)S(1)}, bf16[4,64,256]{2,1,0:T(8,128)(2,1)S(1)}, bf16[4,64,256]{2,1,0:T(8,1...) custom-call(s32[33]{0:T(128)S(1)} %pad_add_fusion.meta_ref, ...), custom_call_target="tpu_custom_call", output_to_operand_aliasing={{4}: (10, {}), {5}: (11, {})} | custom-call | flops 12000000000 | bytes 16777216 | tf_op jit(solution)/shard_map/attn/pallas_call | solution.py:168
  142.8 0.8 collective-permute-done.21.refs_18_.refs_14_
  143.5 1.7 collective-permute-start.20
  145.3 1.1 collective-permute-done.35.refs_2_
  146.3 1.7 collective-permute-start.38
  148.1 0.3 collective-permute-done.36.refs_3_
  148.4 1.9 collective-permute-start.39
  150.3 34.1 %attn.7 = (bf16[8,64,256]{2,1,0:T(8,128)(2,1)S(1)}, bf16[8,64,256]{2,1,0:T(8,128)(2,1)S(1)}, bf16[8,64,256]{2,1,0:T(8,128)(2,1)S(1)}, bf16[8,64,256]{2,1,0:T(8,1...) custom-call(s32[33]{0:T(128)S(1)} %pad_add_fusion.meta_ref, ...), custom_call_target="tpu_custom_call", output_to_operand_aliasing={{4}: (10, {}), {5}: (11, {})} | custom-call | flops 24000000000 | bytes 33554432 | tf_op jit(solution)/shard_map/attn/pallas_call | solution.py:168
  184.4 0.5 collective-permute-start.18
  185.0 0.5 collective-permute-start.2
  185.5 1.1 collective-permute-start.23
  186.6 1.0 collective-permute-start.22
  187.5 34.1 %attn.8 = (bf16[8,64,256]{2,1,0:T(8,128)(2,1)S(1)}, bf16[8,64,256]{2,1,0:T(8,128)(2,1)S(1)}, bf16[8,64,256]{2,1,0:T(8,128)(2,1)S(1)}, bf16[8,64,256]{2,1,0:T(8,1...) custom-call(s32[33]{0:T(128)S(1)} %pad_add_fusion.meta_ref, ...), custom_call_target="tpu_custom_call", output_to_operand_aliasing={{4}: (10, {}), {5}: (11, {})} | custom-call | flops 24000000000 | bytes 33554432 | tf_op jit(solution)/shard_map/attn/pallas_call | solution.py:168
  221.7 0.5 collective-permute-start.24
  222.2 17.2 %collective-permute-done.22.refs_19_.refs_15_ = bf16[656,1024]{1,0:T(8,128)(2,1)S(1)} collective-permute-done((bf16[656,1024]{1,0:T(8,128)(2,1)}, bf16[656,1024]{1,0:T(8,128)(2,1)S(1)}, u32[]{:S(2)}, u32[]{:S(2)}) %collective-permute-start.22) | collective-permute-done | bytes 1343520 | tf_op jit(solution)/shard_map/ppermute | solution.py:331
  239.4 31.6 %attn.9 = (bf16[8,64,256]{2,1,0:T(8,128)(2,1)S(1)}, bf16[8,64,256]{2,1,0:T(8,128)(2,1)S(1)}, bf16[8,64,256]{2,1,0:T(8,128)(2,1)S(1)}, bf16[8,64,256]{2,1,0:T(8,1...) custom-call(s32[33]{0:T(128)S(1)} %pad_add_fusion.meta_ref, ...), custom_call_target="tpu_custom_call", output_to_operand_aliasing={{4}: (10, {}), {5}: (11, {})} | custom-call | flops 24000000000 | bytes 33554432 | tf_op jit(solution)/shard_map/attn/pallas_call | solution.py:168
  271.1 0.5 collective-permute-start.15
  271.6 0.4 collective-permute-start.16
  272.0 1.7 collective-permute-start.32
  273.8 0.9 copy-done.30
  274.8 23.5 %mlp.4.refs_21_ = bf16[32,64,1024]{2,1,0:T(8,128)(2,1)} custom-call(s32[1]{0:T(128)} %bitcast.half_ref, bf16[4,64,256]{2,1,0:T(8,128)(2,1)S(1)} %get-tuple-element.53.refs_0_, bf16[4,64,256]{2,1,0:T(8,128)(2,1)S(1)} %collective-permute-done.34.refs_1_, bf16[4,64,256]{2,1,0:T(8,128)(2,1)S(1)} %collective-permute-done.35.refs_2_, ...), custom_call_target="tpu_custom_call" | custom-call | flops 9663676416 | bytes 23068672 | tf_op jit(solution)/shard_map/mlp/pallas_call | solution.py:289
  298.5 0.9 collective-permute-start.29
  299.4 0.8 collective-permute-start.30
  300.1 23.7 %mlp.5.refs_21_ = bf16[32,64,1024]{2,1,0:T(8,128)(2,1)} custom-call(s32[1]{0:T(128)} %bitcast.half_ref, bf16[8,64,256]{2,1,0:T(8,128)(2,1)S(1)} %get-tuple-element.49.refs_0_, bf16[8,64,256]{2,1,0:T(8,128)(2,1)S(1)} %collective-permute-done.31.refs_1_, bf16[8,64,256]{2,1,0:T(8,128)(2,1)S(1)} %collective-permute-done.32.refs_2_, ...), custom_call_target="tpu_custom_call", output_to_operand_aliasing={{}: (22, {})} | custom-call | flops 9663676416 | bytes 23068672 | tf_op jit(solution)/shard_map/mlp/pallas_call | solution.py:289
  323.8 1.0 collective-permute-start.17
  324.8 23.5 %mlp.6.refs_21_ = bf16[32,64,1024]{2,1,0:T(8,128)(2,1)} custom-call(s32[1]{0:T(128)} %bitcast.half_ref, bf16[8,64,256]{2,1,0:T(8,128)(2,1)S(1)} %get-tuple-element.45.refs_0_, bf16[8,64,256]{2,1,0:T(8,128)(2,1)S(1)} %collective-permute-done.28.refs_1_, bf16[8,64,256]{2,1,0:T(8,128)(2,1)S(1)} %collective-permute-done.29.refs_2_, ...), custom_call_target="tpu_custom_call", output_to_operand_aliasing={{}: (22, {})} | custom-call | flops 9663676416 | bytes 23068672 | tf_op jit(solution)/shard_map/mlp/pallas_call | solution.py:289
  348.3 23.5 %mlp.7 = bf16[32,64,1024]{2,1,0:T(8,128)(2,1)} custom-call(s32[1]{0:T(128)} %bitcast.half_ref, bf16[8,64,256]{2,1,0:T(8,128)(2,1)S(1)} %get-tuple-element.41.refs_0_, bf16[8,64,256]{2,1,0:T(8,128)(2,1)S(1)} %collective-permute-done.15.refs_1_, bf16[8,64,256]{2,1,0:T(8,128)(2,1)S(1)} %collective-permute-done.16.refs_2_, ...), custom_call_target="tpu_custom_call", output_to_operand_aliasing={{}: (22, {})} | custom-call | flops 9663676416 | bytes 23068672 | tf_op jit(solution)/shard_map/mlp/pallas_call | solution.py:289
  (122 shorter events, 1.7 us)
Async XLA Ops:
  5.8 68.5 %collective-permute-start = (bf16[8,64,1024]{2,1,0:T(8,128)(2,1)}, bf16[8,64,1024]{2,1,0:T(8,128)(2,1)S(1)}, u32[]{:S(2)}, u32[]{:S(2)}) collective-permute-start(bf16[8,64,1024]{2,1,0:T(8,128)(2,1)} %ln1.5.a0), channel_id=1, source_target_pairs={{0,1},{1,0},{2,3},{3,2},{4,5},{5,4},{6,7},{7,6}} | collective-permute-start | bytes 3145736 | tf_op jit(solution)/shard_map/ppermute | solution.py:331
  6.7 67.6 %collective-permute-start.1 = (bf16[8,64,1024]{2,1,0:T(8,128)(2,1)}, bf16[8,64,1024]{2,1,0:T(8,128)(2,1)}, u32[]{:S(2)}, u32[]{:S(2)}) collective-permute-start(bf16[8,64,1024]{2,1,0:T(8,128)(2,1)} %ln1.5.a0), channel_id=1, source_target_pairs={{0,2},{2,0},{1,3},{3,1},{4,6},{6,4},{5,7},{7,5}} | collective-permute-start | bytes 3145736 | tf_op jit(solution)/shard_map/ppermute | solution.py:331
  11.4 4.5 %copy-start.22 = (bf16[256,1024]{1,0:T(8,128)(2,1)S(1)}, bf16[256,1024]{1,0:T(8,128)(2,1)}, u32[]{:S(2)}) copy-start(bf16[256,1024]{1,0:T(8,128)(2,1)} %param.24) | copy-start | bytes 1572868
  11.4 16.1 %collective-permute-start.9 = (bf16[4,64,1024]{2,1,0:T(8,128)(2,1)}, bf16[4,64,1024]{2,1,0:T(8,128)(2,1)S(1)}, u32[]{:S(2)}, u32[]{:S(2)}) collective-permute-start(bf16[4,64,1024]{2,1,0:T(8,128)(2,1)} %ln1.8.a0), channel_id=1, source_target_pairs={{0,1},{1,0},{2,3},{3,2},{4,5},{5,4},{6,7},{7,6}} | collective-permute-start | bytes 1572872 | tf_op jit(solution)/shard_map/ppermute | solution.py:331
  11.6 58.7 %collective-permute-start.10 = (bf16[4,64,1024]{2,1,0:T(8,128)(2,1)}, bf16[4,64,1024]{2,1,0:T(8,128)(2,1)}, u32[]{:S(2)}, u32[]{:S(2)}) collective-permute-start(bf16[4,64,1024]{2,1,0:T(8,128)(2,1)} %ln1.8.a0), channel_id=1, source_target_pairs={{0,2},{2,0},{1,3},{3,1},{4,6},{6,4},{5,7},{7,5}} | collective-permute-start | bytes 1572872 | tf_op jit(solution)/shard_map/ppermute | solution.py:331
  14.1 41.6 %collective-permute-start.13 = (bf16[4,64,1024]{2,1,0:T(8,128)(2,1)}, bf16[4,64,1024]{2,1,0:T(8,128)(2,1)}, u32[]{:S(2)}, u32[]{:S(2)}) collective-permute-start(bf16[4,64,1024]{2,1,0:T(8,128)(2,1)} %ln1.9.a0), channel_id=1, source_target_pairs={{0,2},{2,0},{1,3},{3,1},{4,6},{6,4},{5,7},{7,5}} | collective-permute-start | bytes 1572872 | tf_op jit(solution)/shard_map/ppermute | solution.py:331
  15.9 3.6 copy-start.15
  20.7 6.8 %copy-start.11 = (bf16[1,512,1024]{2,1,0:T(8,128)(2,1)}, bf16[1,512,1024]{2,1,0:T(8,128)(2,1)S(1)}, u32[]{:S(2)}) copy-start(bf16[1,512,1024]{2,1,0:T(8,128)(2,1)S(1)} %get-tuple-element.63) | copy-start | bytes 3145732
  20.7 2.1 copy-start.19
  20.7 2.2 copy-start.20
  22.3 5.9 %copy-start.4 = (bf16[4,64,1024]{2,1,0:T(8,128)(2,1)S(1)}, bf16[4,64,1024]{2,1,0:T(8,128)(2,1)}, u32[]{:S(2)}) copy-start(bf16[4,64,1024]{2,1,0:T(8,128)(2,1)} %ln1.9.a0) | copy-start | bytes 1572868
  22.3 33.4 %copy-start.33 = (s32[32]{0:T(128)S(1)}, s32[32]{0:T(128)}, u32[]{:S(2)}) copy-start(s32[32]{0:T(128)} %param.17) | copy-start | bytes 388
  27.5 30.1 %copy-start.24 = (bf16[768]{0:T(1024)(128)(2,1)S(1)}, bf16[768]{0:T(1024)(128)(2,1)}, u32[]{:S(2)}) copy-start(bf16[768]{0:T(1024)(128)(2,1)} %param.23) | copy-start | bytes 4612
  27.5 30.3 %copy-start.25 = (bf16[1024]{0:T(1024)(128)(2,1)S(1)}, bf16[1024]{0:T(1024)(128)(2,1)}, u32[]{:S(2)}) copy-start(bf16[1024]{0:T(1024)(128)(2,1)} %param.25) | copy-start | bytes 6148
  28.3 44.3 %collective-permute-start.12 = (bf16[4,64,1024]{2,1,0:T(8,128)(2,1)S(1)}, bf16[4,64,1024]{2,1,0:T(8,128)(2,1)}, u32[]{:S(2)}, u32[]{:S(2)}) collective-permute-start(bf16[4,64,1024]{2,1,0:T(8,128)(2,1)S(1)} %copy-done.4), channel_id=1, source_target_pairs={{0,1},{1,0},{2,3},{3,2},{4,5},{5,4},{6,7},{7,6}} | collective-permute-start | bytes 1572872 | tf_op jit(solution)/shard_map/ppermute | solution.py:331
  55.8 19.6 %collective-permute-start.14 = (bf16[4,64,1024]{2,1,0:T(8,128)(2,1)}, bf16[4,64,1024]{2,1,0:T(8,128)(2,1)}, u32[]{:S(2)}, u32[]{:S(2)}) collective-permute-start(bf16[4,64,1024]{2,1,0:T(8,128)(2,1)} %collective-permute-done.13.a2), channel_id=1, source_target_pairs={{0,1},{1,0},{2,3},{3,2},{4,5},{5,4},{6,7},{7,6}} | collective-permute-start | bytes 1572872 | tf_op jit(solution)/shard_map/ppermute | solution.py:331
  70.0 114.9 %copy-start.16 = (bf16[2,512,1024]{2,1,0:T(8,128)(2,1)}, bf16[2,512,1024]{2,1,0:T(8,128)(2,1)S(1)}, u32[]{:S(2)}) copy-start(bf16[2,512,1024]{2,1,0:T(8,128)(2,1)S(1)} %pad_maximum_fusion.1.refs_14_.refs_10_) | copy-start | bytes 6291460
  70.0 2.0 copy-start.1
  70.0 4.2 %copy-start.2 = (bf16[8,64,1024]{2,1,0:T(8,128)(2,1)S(1)}, bf16[8,64,1024]{2,1,0:T(8,128)(2,1)}, u32[]{:S(2)}) copy-start(bf16[8,64,1024]{2,1,0:T(8,128)(2,1)} %ln1.7.a0) | copy-start | bytes 3145732
  70.3 114.1 %copy-start.14 = (bf16[2,656,1024]{2,1,0:T(8,128)(2,1)}, bf16[2,656,1024]{2,1,0:T(8,128)(2,1)S(1)}, u32[]{:S(2)}) copy-start(bf16[2,656,1024]{2,1,0:T(8,128)(2,1)S(1)} %pad_maximum_fusion.refs_13_.refs_9_) | copy-start | bytes 8060932
  72.0 23.0 %collective-permute-start.3 = (bf16[8,64,1024]{2,1,0:T(8,128)(2,1)S(1)}, bf16[8,64,1024]{2,1,0:T(8,128)(2,1)S(1)}, u32[]{:S(2)}, u32[]{:S(2)}) collective-permute-start(bf16[8,64,1024]{2,1,0:T(8,128)(2,1)S(1)} %copy-done.1), channel_id=1, source_target_pairs={{0,1},{1,0},{2,3},{3,2},{4,5},{5,4},{6,7},{7,6}} | collective-permute-start | bytes 3145736 | tf_op jit(solution)/shard_map/ppermute | solution.py:331
  72.5 26.0 %collective-permute-start.4 = (bf16[8,64,1024]{2,1,0:T(8,128)(2,1)S(1)}, bf16[8,64,1024]{2,1,0:T(8,128)(2,1)S(1)}, u32[]{:S(2)}, u32[]{:S(2)}) collective-permute-start(bf16[8,64,1024]{2,1,0:T(8,128)(2,1)S(1)} %copy-done.1), channel_id=1, source_target_pairs={{0,2},{2,0},{1,3},{3,1},{4,6},{6,4},{5,7},{7,5}} | collective-permute-start | bytes 3145736 | tf_op jit(solution)/shard_map/ppermute | solution.py:331
  74.3 24.3 %collective-permute-start.6 = (bf16[8,64,1024]{2,1,0:T(8,128)(2,1)S(1)}, bf16[8,64,1024]{2,1,0:T(8,128)(2,1)S(1)}, u32[]{:S(2)}, u32[]{:S(2)}) collective-permute-start(bf16[8,64,1024]{2,1,0:T(8,128)(2,1)S(1)} %copy-done.2), channel_id=1, source_target_pairs={{0,1},{1,0},{2,3},{3,2},{4,5},{5,4},{6,7},{7,6}} | collective-permute-start | bytes 3145736 | tf_op jit(solution)/shard_map/ppermute | solution.py:331
  74.3 46.7 %collective-permute-start.7 = (bf16[8,64,1024]{2,1,0:T(8,128)(2,1)S(1)}, bf16[8,64,1024]{2,1,0:T(8,128)(2,1)S(1)}, u32[]{:S(2)}, u32[]{:S(2)}) collective-permute-start(bf16[8,64,1024]{2,1,0:T(8,128)(2,1)S(1)} %copy-done.2), channel_id=1, source_target_pairs={{0,2},{2,0},{1,3},{3,1},{4,6},{6,4},{5,7},{7,5}} | collective-permute-start | bytes 3145736 | tf_op jit(solution)/shard_map/ppermute | solution.py:331
  75.4 45.7 %collective-permute-start.11 = (bf16[4,64,1024]{2,1,0:T(8,128)(2,1)}, bf16[4,64,1024]{2,1,0:T(8,128)(2,1)S(1)}, u32[]{:S(2)}, u32[]{:S(2)}) collective-permute-start(bf16[4,64,1024]{2,1,0:T(8,128)(2,1)} %collective-permute-done.10.a2), channel_id=1, source_target_pairs={{0,1},{1,0},{2,3},{3,2},{4,5},{5,4},{6,7},{7,6}} | collective-permute-start | bytes 1572872 | tf_op jit(solution)/shard_map/ppermute | solution.py:331
  75.4 19.6 %copy-start.21 = (bf16[512,1024]{1,0:T(8,128)(2,1)S(1)}, bf16[512,1024]{1,0:T(8,128)(2,1)}, u32[]{:S(2)}) copy-start(bf16[512,1024]{1,0:T(8,128)(2,1)} %fusion.8) | copy-start | bytes 3145732
  75.4 47.5 %copy-start.3 = (bf16[4,64,1024]{2,1,0:T(8,128)(2,1)S(1)}, bf16[4,64,1024]{2,1,0:T(8,128)(2,1)}, u32[]{:S(2)}) copy-start(bf16[4,64,1024]{2,1,0:T(8,128)(2,1)} %ln1.8.a0) | copy-start | bytes 1572868
  75.4 47.5 %copy-start.6 = (bf16[4,64,1024]{2,1,0:T(8,128)(2,1)S(1)}, bf16[4,64,1024]{2,1,0:T(8,128)(2,1)}, u32[]{:S(2)}) copy-start(bf16[4,64,1024]{2,1,0:T(8,128)(2,1)} %copy-done.5) | copy-start | bytes 1572868
  95.0 48.5 %collective-permute-start.21 = (bf16[512,1024]{1,0:T(8,128)(2,1)S(1)}, bf16[512,1024]{1,0:T(8,128)(2,1)S(1)}, u32[]{:S(2)}, u32[]{:S(2)}) collective-permute-start(bf16[512,1024]{1,0:T(8,128)(2,1)S(1)} %copy-done.21), channel_id=1, source_target_pairs={{0,2},{2,0},{1,3},{3,1},{4,6},{6,4},{5,7},{7,5}} | collective-permute-start | bytes 3145736 | tf_op jit(solution)/shard_map/ppermute | solution.py:331
  98.6 46.7 %collective-permute-start.34 = (bf16[4,64,256]{2,1,0:T(8,128)(2,1)S(1)}, bf16[4,64,256]{2,1,0:T(8,128)(2,1)S(1)}, u32[]{:S(2)}, u32[]{:S(2)}) collective-permute-start(bf16[4,64,256]{2,1,0:T(8,128)(2,1)S(1)} %get-tuple-element.54), channel_id=1, source_target_pairs={{0,1},{1,0},{2,3},{3,2},{4,5},{5,4},{6,7},{7,6}} | collective-permute-start | bytes 393224 | tf_op jit(solution)/shard_map/ppermute | solution.py:331
  98.6 47.7 %collective-permute-start.35 = (bf16[4,64,256]{2,1,0:T(8,128)(2,1)S(1)}, bf16[4,64,256]{2,1,0:T(8,128)(2,1)S(1)}, u32[]{:S(2)}, u32[]{:S(2)}) collective-permute-start(bf16[4,64,256]{2,1,0:T(8,128)(2,1)S(1)} %get-tuple-element.55), channel_id=1, source_target_pairs={{0,2},{2,0},{1,3},{3,1},{4,6},{6,4},{5,7},{7,5}} | collective-permute-start | bytes 393224 | tf_op jit(solution)/shard_map/ppermute | solution.py:331
  121.0 27.3 %collective-permute-start.36 = (bf16[4,64,256]{2,1,0:T(8,128)(2,1)S(1)}, bf16[4,64,256]{2,1,0:T(8,128)(2,1)S(1)}, u32[]{:S(2)}, u32[]{:S(2)}) collective-permute-start(bf16[4,64,256]{2,1,0:T(8,128)(2,1)S(1)} %get-tuple-element.56), channel_id=1, source_target_pairs={{0,3},{3,0},{1,2},{2,1},{4,7},{7,4},{5,6},{6,5}} | collective-permute-start | bytes 393224 | tf_op jit(solution)/shard_map/ppermute | solution.py:331
  121.1 29.3 %collective-permute-start.8 = (bf16[8,64,1024]{2,1,0:T(8,128)(2,1)S(1)}, bf16[8,64,1024]{2,1,0:T(8,128)(2,1)S(1)}, u32[]{:S(2)}, u32[]{:S(2)}) collective-permute-start(bf16[8,64,1024]{2,1,0:T(8,128)(2,1)S(1)} %collective-permute-done.7.a2), channel_id=1, source_target_pairs={{0,1},{1,0},{2,3},{3,2},{4,5},{5,4},{6,7},{7,6}} | collective-permute-start | bytes 3145736 | tf_op jit(solution)/shard_map/ppermute | solution.py:331
  143.5 78.1 %copy-start.31 = (bf16[512,1024]{1,0:T(8,128)(2,1)}, bf16[512,1024]{1,0:T(8,128)(2,1)S(1)}, u32[]{:S(2)}) copy-start(bf16[512,1024]{1,0:T(8,128)(2,1)S(1)} %collective-permute-done.21.refs_18_.refs_14_) | copy-start | bytes 3145732
  143.5 42.0 %collective-permute-start.20 = (bf16[656,1024]{1,0:T(8,128)(2,1)S(1)}, bf16[656,1024]{1,0:T(8,128)(2,1)}, u32[]{:S(2)}, u32[]{:S(2)}) collective-permute-start(bf16[656,1024]{1,0:T(8,128)(2,1)S(1)} %fusion.6), channel_id=1, source_target_pairs={{0,2},{2,0},{1,3},{3,1},{4,6},{6,4},{5,7},{7,5}} | collective-permute-start | bytes 4030472 | tf_op jit(solution)/shard_map/ppermute | solution.py:331
  145.3 39.2 %collective-permute-start.37 = (bf16[4,64,256]{2,1,0:T(8,128)(2,1)S(1)}, bf16[4,64,256]{2,1,0:T(8,128)(2,1)S(1)}, u32[]{:S(2)}, u32[]{:S(2)}) collective-permute-start(bf16[4,64,256]{2,1,0:T(8,128)(2,1)S(1)} %get-tuple-element.58), channel_id=1, source_target_pairs={{0,1},{1,0},{2,3},{3,2},{4,5},{5,4},{6,7},{7,6}} | collective-permute-start | bytes 393224 | tf_op jit(solution)/shard_map/ppermute | solution.py:331
  146.3 38.6 %collective-permute-start.38 = (bf16[4,64,256]{2,1,0:T(8,128)(2,1)S(1)}, bf16[4,64,256]{2,1,0:T(8,128)(2,1)S(1)}, u32[]{:S(2)}, u32[]{:S(2)}) collective-permute-start(bf16[4,64,256]{2,1,0:T(8,128)(2,1)S(1)} %get-tuple-element.59), channel_id=1, source_target_pairs={{0,2},{2,0},{1,3},{3,1},{4,6},{6,4},{5,7},{7,5}} | collective-permute-start | bytes 393224 | tf_op jit(solution)/shard_map/ppermute | solution.py:331
  148.4 36.6 %collective-permute-start.39 = (bf16[4,64,256]{2,1,0:T(8,128)(2,1)S(1)}, bf16[4,64,256]{2,1,0:T(8,128)(2,1)S(1)}, u32[]{:S(2)}, u32[]{:S(2)}) collective-permute-start(bf16[4,64,256]{2,1,0:T(8,128)(2,1)S(1)} %get-tuple-element.60), channel_id=1, source_target_pairs={{0,3},{3,0},{1,2},{2,1},{4,7},{7,4},{5,6},{6,5}} | collective-permute-start | bytes 393224 | tf_op jit(solution)/shard_map/ppermute | solution.py:331
  150.3 36.3 %collective-permute-start.5 = (bf16[8,64,1024]{2,1,0:T(8,128)(2,1)S(1)}, bf16[8,64,1024]{2,1,0:T(8,128)(2,1)S(1)}, u32[]{:S(2)}, u32[]{:S(2)}) collective-permute-start(bf16[8,64,1024]{2,1,0:T(8,128)(2,1)S(1)} %collective-permute-done.4.a2), channel_id=1, source_target_pairs={{0,1},{1,0},{2,3},{3,2},{4,5},{5,4},{6,7},{7,6}} | collective-permute-start | bytes 3145736 | tf_op jit(solution)/shard_map/ppermute | solution.py:331
  184.4 87.1 %collective-permute-start.18 = (bf16[2,656,1024]{2,1,0:T(8,128)(2,1)S(1)}, bf16[2,656,1024]{2,1,0:T(8,128)(2,1)S(1)}, u32[]{:S(2)}, u32[]{:S(2)}) collective-permute-start(bf16[2,656,1024]{2,1,0:T(8,128)(2,1)S(1)} %pad_maximum_fusion.refs_13_.refs_9_), channel_id=1, source_target_pairs={{0,1},{1,0},{2,3},{3,2},{4,5},{5,4},{6,7},{7,6}} | collective-permute-start | bytes 8060936 | tf_op jit(solution)/shard_map/ppermute | solution.py:331
  185.0 36.7 %collective-permute-start.19 = (bf16[2,512,1024]{2,1,0:T(8,128)(2,1)S(1)}, bf16[2,512,1024]{2,1,0:T(8,128)(2,1)}, u32[]{:S(2)}, u32[]{:S(2)}) collective-permute-start(bf16[2,512,1024]{2,1,0:T(8,128)(2,1)S(1)} %pad_maximum_fusion.1.refs_14_.refs_10_), channel_id=1, source_target_pairs={{0,1},{1,0},{2,3},{3,2},{4,5},{5,4},{6,7},{7,6}} | collective-permute-start | bytes 6291464 | tf_op jit(solution)/shard_map/ppermute | solution.py:331
  185.0 36.6 %collective-permute-start.2 = (bf16[8,64,1024]{2,1,0:T(8,128)(2,1)}, bf16[8,64,1024]{2,1,0:T(8,128)(2,1)S(1)}, u32[]{:S(2)}, u32[]{:S(2)}) collective-permute-start(bf16[8,64,1024]{2,1,0:T(8,128)(2,1)} %collective-permute-done.1.a2), channel_id=1, source_target_pairs={{0,1},{1,0},{2,3},{3,2},{4,5},{5,4},{6,7},{7,6}} | collective-permute-start | bytes 3145736 | tf_op jit(solution)/shard_map/ppermute | solution.py:331
  185.5 36.7 %collective-permute-start.23 = (bf16[512,1024]{1,0:T(8,128)(2,1)S(1)}, bf16[512,1024]{1,0:T(8,128)(2,1)}, u32[]{:S(2)}, u32[]{:S(2)}) collective-permute-start(bf16[512,1024]{1,0:T(8,128)(2,1)S(1)} %collective-permute-done.21.refs_18_.refs_14_), channel_id=1, source_target_pairs={{0,4},{4,0},{1,5},{5,1},{2,6},{6,2},{3,7},{7,3}} | collective-permute-start | bytes 3145736 | tf_op jit(solution)/shard_map/ppermute | solution.py:331
  186.6 52.8 %collective-permute-start.22 = (bf16[656,1024]{1,0:T(8,128)(2,1)}, bf16[656,1024]{1,0:T(8,128)(2,1)S(1)}, u32[]{:S(2)}, u32[]{:S(2)}) collective-permute-start(bf16[656,1024]{1,0:T(8,128)(2,1)} %collective-permute-done.20.refs_17_.refs_13_), channel_id=1, source_target_pairs={{0,4},{4,0},{1,5},{5,1},{2,6},{6,2},{3,7},{7,3}} | collective-permute-start | bytes 4030472 | tf_op jit(solution)/shard_map/ppermute | solution.py:331
  187.5 51.9 %copy-start = (bf16[8,64,1024]{2,1,0:T(8,128)(2,1)S(1)}, bf16[8,64,1024]{2,1,0:T(8,128)(2,1)}, u32[]{:S(2)}) copy-start(bf16[8,64,1024]{2,1,0:T(8,128)(2,1)} %ln1.5.a0) | copy-start | bytes 3145732
  221.6 49.4 %collective-permute-start.25 = (bf16[512,1024]{1,0:T(8,128)(2,1)S(1)}, bf16[512,1024]{1,0:T(8,128)(2,1)}, u32[]{:S(2)}, u32[]{:S(2)}) collective-permute-start(bf16[512,1024]{1,0:T(8,128)(2,1)S(1)} %collective-permute-done.21.refs_18_.refs_14_), channel_id=1, source_target_pairs={{0,1},{1,0},{2,3},{3,2},{4,5},{5,4},{6,7},{7,6}} | collective-permute-start | bytes 3145736 | tf_op jit(solution)/shard_map/ppermute | solution.py:331
  221.7 50.3 %collective-permute-start.24 = (bf16[656,1024]{1,0:T(8,128)(2,1)}, bf16[656,1024]{1,0:T(8,128)(2,1)S(1)}, u32[]{:S(2)}, u32[]{:S(2)}) collective-permute-start(bf16[656,1024]{1,0:T(8,128)(2,1)} %collective-permute-done.20.refs_17_.refs_13_), channel_id=1, source_target_pairs={{0,1},{1,0},{2,3},{3,2},{4,5},{5,4},{6,7},{7,6}} | collective-permute-start | bytes 4030472 | tf_op jit(solution)/shard_map/ppermute | solution.py:331
  222.2 49.8 %collective-permute-start.27 = (bf16[512,1024]{1,0:T(8,128)(2,1)}, bf16[512,1024]{1,0:T(8,128)(2,1)S(1)}, u32[]{:S(2)}, u32[]{:S(2)}) collective-permute-start(bf16[512,1024]{1,0:T(8,128)(2,1)} %collective-permute-done.23.refs_20_.refs_16_), channel_id=1, source_target_pairs={{0,1},{1,0},{2,3},{3,2},{4,5},{5,4},{6,7},{7,6}} | collective-permute-start | bytes 3145736 | tf_op jit(solution)/shard_map/ppermute | solution.py:331
  239.4 31.6 %copy-start.28 = (bf16[656,1024]{1,0:T(8,128)(2,1)}, bf16[656,1024]{1,0:T(8,128)(2,1)S(1)}, u32[]{:S(2)}) copy-start(bf16[656,1024]{1,0:T(8,128)(2,1)S(1)} %collective-permute-done.22.refs_19_.refs_15_) | copy-start | bytes 4030468
  239.4 34.2 %collective-permute-start.26 = (bf16[656,1024]{1,0:T(8,128)(2,1)S(1)}, bf16[656,1024]{1,0:T(8,128)(2,1)S(1)}, u32[]{:S(2)}, u32[]{:S(2)}) collective-permute-start(bf16[656,1024]{1,0:T(8,128)(2,1)S(1)} %collective-permute-done.22.refs_19_.refs_15_), channel_id=1, source_target_pairs={{0,1},{1,0},{2,3},{3,2},{4,5},{5,4},{6,7},{7,6}} | collective-permute-start | bytes 4030472 | tf_op jit(solution)/shard_map/ppermute | solution.py:331
  239.4 35.3 %copy-start.7 = (bf16[1,1024]{1,0:T(2,128)(2,1)S(1)}, bf16[1,1024]{1,0:T(2,128)(2,1)}, u32[]{:S(2)}) copy-start(bf16[1,1024]{1,0:T(2,128)(2,1)} %reshape.49.refs_11_.refs_7_) | copy-start | bytes 6148
  239.4 35.3 %copy-start.8 = (bf16[1,1024]{1,0:T(2,128)(2,1)S(1)}, bf16[1,1024]{1,0:T(2,128)(2,1)}, u32[]{:S(2)}) copy-start(bf16[1,1024]{1,0:T(2,128)(2,1)} %reshape.50.refs_12_.refs_8_) | copy-start | bytes 6148
  271.1 77.2 %collective-permute-start.15 = (bf16[8,64,256]{2,1,0:T(8,128)(2,1)S(1)}, bf16[8,64,256]{2,1,0:T(8,128)(2,1)S(1)}, u32[]{:S(2)}, u32[]{:S(2)}) collective-permute-start(bf16[8,64,256]{2,1,0:T(8,128)(2,1)S(1)} %get-tuple-element.42), channel_id=1, source_target_pairs={{0,1},{1,0},{2,3},{3,2},{4,5},{5,4},{6,7},{7,6}} | collective-permute-start | bytes 786440 | tf_op jit(solution)/shard_map/ppermute | solution.py:331
  271.6 2.2 copy-start.27
  271.6 76.8 %collective-permute-start.16 = (bf16[8,64,256]{2,1,0:T(8,128)(2,1)S(1)}, bf16[8,64,256]{2,1,0:T(8,128)(2,1)S(1)}, u32[]{:S(2)}, u32[]{:S(2)}) collective-permute-start(bf16[8,64,256]{2,1,0:T(8,128)(2,1)S(1)} %get-tuple-element.43), channel_id=1, source_target_pairs={{0,2},{2,0},{1,3},{3,1},{4,6},{6,4},{5,7},{7,5}} | collective-permute-start | bytes 786440 | tf_op jit(solution)/shard_map/ppermute | solution.py:331
  271.9 2.8 copy-start.29
  271.9 26.3 %collective-permute-start.31 = (bf16[8,64,256]{2,1,0:T(8,128)(2,1)S(1)}, bf16[8,64,256]{2,1,0:T(8,128)(2,1)S(1)}, u32[]{:S(2)}, u32[]{:S(2)}) collective-permute-start(bf16[8,64,256]{2,1,0:T(8,128)(2,1)S(1)} %get-tuple-element.50), channel_id=1, source_target_pairs={{0,1},{1,0},{2,3},{3,2},{4,5},{5,4},{6,7},{7,6}} | collective-permute-start | bytes 786440 | tf_op jit(solution)/shard_map/ppermute | solution.py:331
  271.9 2.8 copy-start.32
  272.0 26.5 %collective-permute-start.32 = (bf16[8,64,256]{2,1,0:T(8,128)(2,1)S(1)}, bf16[8,64,256]{2,1,0:T(8,128)(2,1)S(1)}, u32[]{:S(2)}, u32[]{:S(2)}) collective-permute-start(bf16[8,64,256]{2,1,0:T(8,128)(2,1)S(1)} %get-tuple-element.51), channel_id=1, source_target_pairs={{0,2},{2,0},{1,3},{3,1},{4,6},{6,4},{5,7},{7,5}} | collective-permute-start | bytes 786440 | tf_op jit(solution)/shard_map/ppermute | solution.py:331
  273.6 25.7 %collective-permute-start.33 = (bf16[8,64,256]{2,1,0:T(8,128)(2,1)S(1)}, bf16[8,64,256]{2,1,0:T(8,128)(2,1)S(1)}, u32[]{:S(2)}, u32[]{:S(2)}) collective-permute-start(bf16[8,64,256]{2,1,0:T(8,128)(2,1)S(1)} %get-tuple-element.52), channel_id=1, source_target_pairs={{0,3},{3,0},{1,2},{2,1},{4,7},{7,4},{5,6},{6,5}} | collective-permute-start | bytes 786440 | tf_op jit(solution)/shard_map/ppermute | solution.py:331
  298.3 25.6 %collective-permute-start.28 = (bf16[8,64,256]{2,1,0:T(8,128)(2,1)S(1)}, bf16[8,64,256]{2,1,0:T(8,128)(2,1)S(1)}, u32[]{:S(2)}, u32[]{:S(2)}) collective-permute-start(bf16[8,64,256]{2,1,0:T(8,128)(2,1)S(1)} %get-tuple-element.46), channel_id=1, source_target_pairs={{0,1},{1,0},{2,3},{3,2},{4,5},{5,4},{6,7},{7,6}} | collective-permute-start | bytes 786440 | tf_op jit(solution)/shard_map/ppermute | solution.py:331
  298.5 26.4 %collective-permute-start.29 = (bf16[8,64,256]{2,1,0:T(8,128)(2,1)S(1)}, bf16[8,64,256]{2,1,0:T(8,128)(2,1)S(1)}, u32[]{:S(2)}, u32[]{:S(2)}) collective-permute-start(bf16[8,64,256]{2,1,0:T(8,128)(2,1)S(1)} %get-tuple-element.47), channel_id=1, source_target_pairs={{0,2},{2,0},{1,3},{3,1},{4,6},{6,4},{5,7},{7,5}} | collective-permute-start | bytes 786440 | tf_op jit(solution)/shard_map/ppermute | solution.py:331
  299.4 25.5 %collective-permute-start.30 = (bf16[8,64,256]{2,1,0:T(8,128)(2,1)S(1)}, bf16[8,64,256]{2,1,0:T(8,128)(2,1)S(1)}, u32[]{:S(2)}, u32[]{:S(2)}) collective-permute-start(bf16[8,64,256]{2,1,0:T(8,128)(2,1)S(1)} %get-tuple-element.48), channel_id=1, source_target_pairs={{0,3},{3,0},{1,2},{2,1},{4,7},{7,4},{5,6},{6,5}} | collective-permute-start | bytes 786440 | tf_op jit(solution)/shard_map/ppermute | solution.py:331
  323.8 24.5 %collective-permute-start.17 = (bf16[8,64,256]{2,1,0:T(8,128)(2,1)S(1)}, bf16[8,64,256]{2,1,0:T(8,128)(2,1)S(1)}, u32[]{:S(2)}, u32[]{:S(2)}) collective-permute-start(bf16[8,64,256]{2,1,0:T(8,128)(2,1)S(1)} %get-tuple-element.44), channel_id=1, source_target_pairs={{0,3},{3,0},{1,2},{2,1},{4,7},{7,4},{5,6},{6,5}} | collective-permute-start | bytes 786440 | tf_op jit(solution)/shard_map/ppermute | solution.py:331
  (10 other events, 14.9 us)
